TPU v7x, 32 devices: a whole 2x2x4 slice. The times are simulated.
32 devices in a mesh: hw: 8 (over y, x, core), head: 4 (over z).
Axes of the slice: x: 2, y: 2, z: 4, core: 2. Of those that a mesh axis runs over, the one named last changes fastest.
Arguments:
- latents: bfloat16 [8, 8, 8, 8, 5120], P('hw'), may hold values from -6 to 6
- query_weight: bfloat16 [5120, 2560], P('hw', 'head'), may hold values from -0.125 to 0.125
- key_weight: bfloat16 [5120, 2560], P('hw', 'head'), may hold values from -0.125 to 0.125
- value_weight: bfloat16 [5120, 2560], P('hw', 'head'), may hold values from -0.078125 to 0.078125
- output_weight: bfloat16 [2560, 5120], P('hw', 'head'), may hold values from -0.5 to 0.5
- query_gain: float32 [2560], P('head'), may hold values from 0.3 to 9
- key_gain: float32 [2560], P('head'), may hold values from 0.3 to 9
- frame_index: int32 [8], replicated, may hold values from 0 to 94, as said below
- row_index: int32 [32], replicated, may hold values from 0 to 286, as said below
- column_index: int32 [16], replicated, may hold values from 0 to 158, as said below
Outputs:
- attention_out: bfloat16 [8, 8, 8, 8, 5120], P('hw', None, None, None, 'head')
Inputs may be any that keep to these rules, and one draw needn't show every extreme that they name: `frame_index`: strictly increasing. `row_index`: strictly increasing. `column_index`: strictly increasing.
All inputs are finite; a program needn't handle non-finite values.
Results may differ from a plain program's by a relative error of at most 0.0075.
The roundings to bfloat16 on the way count: a program that leaves them out, or rounds other values in their place, can miss the bound.
Values may be sent and summed in bfloat16 or wider, within the bound.
A program may use at most 128 MiB of HBM per device.

v0:
```python
import functools
import math

import jax
import jax.numpy as jnp
from jax import lax
from jax.experimental import pallas as pl
from jax.experimental.pallas import tpu as pltpu
from jax.sharding import PartitionSpec as P

HEADS = 20
HD = 128
WT = 4
DEV_ROWS = 4


NORM_EPS = 0.5


def freq_table(count):
    ratios = jnp.arange(count, dtype=jnp.float32) / count
    return jnp.float32(10000.0) ** (-ratios)


def rope_angles(frame_index, row_index, column_index, head_dim):
    side_pairs = head_dim // 6
    frame_pairs = head_dim // 2 - 2 * side_pairs

    def lanes(before, count, after):
        return jnp.repeat(jnp.pad(freq_table(count), (before, after)), 2)

    frame_part = frame_index.astype(jnp.float32)[:, None] * lanes(0, frame_pairs, 2 * side_pairs)
    row_part = row_index.astype(jnp.float32)[:, None] * lanes(frame_pairs, side_pairs, side_pairs)
    column_part = column_index.astype(jnp.float32)[:, None] * lanes(
        frame_pairs + side_pairs, side_pairs, 0
    )
    total = frame_part[:, None, None] + row_part[:, None] + column_part
    return total.reshape(-1, head_dim)


def rotate(features, cosine, sine, heads_here, head_dim):
    even = lax.broadcasted_iota(jnp.int32, cosine.shape, 1) % 2 == 0
    heads = []
    for head in range(heads_here):
        one = features[:, head * head_dim : (head + 1) * head_dim]
        turned = jnp.where(even, -jnp.roll(one, -1, axis=1), jnp.roll(one, 1, axis=1))
        heads.append((one * cosine + turned * sine).astype(jnp.bfloat16))
    return jnp.concatenate(heads, axis=1)


CUBE = 8


class Cube:
    def __init__(self, stride):
        me = lax.axis_index("hw")
        within = lax.rem(me, stride) if stride > 1 else 0
        place = lax.div(me, stride) if stride > 1 else me
        core = lax.rem(place, 2)
        x = lax.rem(lax.div(place, 2), 2)
        y = lax.div(place, 4)
        self.place = place
        self.other = [place + 1 - 2 * core, place + 2 - 4 * x, place + 4 - 8 * y]
        self.diagonal = place + 2 - 4 * x + 4 - 8 * y
        self.devices = [{"hw": other * stride + within} for other in self.other]
        self.chip = lax.div(place, 2)
        self.chips = [
            self.chip,
            self.chip + 1 - 2 * x,
            self.chip + 2 - 4 * y,
            self.chip + 3 - 2 * x - 4 * y,
        ]

    def barrier(self, line=None):
        semaphore = pltpu.get_barrier_semaphore()
        if line is not None:
            for peers in line:
                peers.greet(semaphore)
        for device in self.devices:
            pl.semaphore_signal(semaphore, inc=1, device_id=device, device_id_type=pl.DeviceIdType.MESH)
        if line is None:
            pl.semaphore_wait(semaphore, len(self.devices))
        else:
            count = sum((peers.number() for peers in line), len(self.devices))
            pl.semaphore_wait(semaphore, count)


class Exchange:
    def __init__(self, cube, held, send, receive, rows):
        core_place, x_place, y_place = cube.other
        half = rows // 2

        def part(place, low, size):
            start = pl.multiple_of(lax.rem(place, 2) * rows + low, 16)
            return held.at[lax.div(place, 2), pl.ds(start, size)]

        def copy(at, place, low, size, partner):
            ref = part(place, low, size)
            return pltpu.make_async_remote_copy(
                src_ref=ref,
                dst_ref=ref,
                send_sem=send.at[at],
                recv_sem=receive.at[at],
                device_id=cube.devices[partner],
                device_id_type=pl.DeviceIdType.MESH,
            )

        self.own = part(cube.place, 0, rows)
        self.copies = [
            copy(0, cube.place, 0, rows, 1),
            copy(1, cube.place, 0, rows, 2),
            copy(2, cube.place, 0, rows, 0),
            copy(3, x_place, 0, rows, 0),
            copy(4, y_place, 0, rows, 0),
            copy(5, x_place, 0, half, 2),
            copy(6, y_place, half, half, 1),
            copy(7, cube.diagonal, 0, half, 0),
            copy(8, cube.diagonal, half, half, 0),
        ]

    def start(self, *which):
        for at in which:
            self.copies[at].start()

    def arrived(self, *which):
        for at in which:
            self.copies[at].wait_recv()

    def near(self):
        self.arrived(0)
        self.start(5, 3)
        self.arrived(1)
        self.start(6, 4)

    def far(self):
        self.arrived(5)
        self.start(7)
        self.arrived(6)
        self.start(8)

    def sent(self):
        for one in self.copies:
            one.wait_send()


class Peers:
    def __init__(self, parts, send, receive):
        self.count = lax.axis_size("head")
        self.me = lax.axis_index("head")
        self.parts, self.send, self.receive = parts, send, receive

    def device(self, step):
        return {"head": lax.rem(self.me + step, self.count)}

    def greet(self, semaphore):
        for step in range(1, self.count):
            pl.semaphore_signal(
                semaphore,
                inc=1,
                device_id=self.device(step),
                device_id_type=pl.DeviceIdType.MESH,
            )

    def number(self):
        return self.count - 1

    def copy(self, step, group):
        ref = self.parts.at[group]
        return pltpu.make_async_remote_copy(
            src_ref=ref,
            dst_ref=ref,
            send_sem=self.send.at[step - 1],
            recv_sem=self.receive.at[step - 1],
            device_id=self.device(step),
            device_id_type=pl.DeviceIdType.MESH,
        )

    def start(self):
        for step in range(1, self.count):
            self.copy(step, self.me).start()

    def finish(self):
        for step in range(1, self.count):
            self.copy(step, lax.rem(self.me + self.count - step, self.count)).wait_recv()

    def sent(self):
        for step in range(1, self.count):
            self.copy(step, self.me).wait_send()


def project_kernel(
    stride, tokens_hbm, query_hbm, key_hbm, value_hbm,
    query_ref, key_ref, value_ref, squares_ref,
    tokens, held, value_sum, parts, local, send, receive, parts_send, parts_receive,
):
    cube = Cube(stride)
    rows = query_hbm.shape[0]
    depth = 2 * rows
    weights = [
        Exchange(cube, held.at[at], send.at[at], receive.at[at], rows) for at in range(3)
    ]
    loads = [
        pltpu.make_async_copy(source, weight.own, local.at[at])
        for at, (source, weight) in enumerate(
            zip((query_hbm, key_hbm, value_hbm), weights)
        )
    ]
    fetch = pltpu.make_async_copy(tokens_hbm, tokens, local.at[3])
    for load in loads:
        load.start()
    fetch.start()
    peers = Peers(parts, parts_send, parts_receive)
    cube.barrier((peers,))
    query, key, value = weights
    loads[0].wait()
    query.start(2, 0, 1)
    loads[1].wait()
    key.start(2, 0, 1)
    sums = [query_ref, key_ref, value_sum]
    block = tokens.shape[0] // 2

    def multiply(at, lane):
        chip = cube.chips[lane]

        @pl.loop(0, 2)
        def _(step):
            here = pl.ds(pl.multiple_of(step * block, block), block)
            product = jnp.dot(
                tokens[here, pl.ds(pl.multiple_of(chip * depth, 128), depth)],
                held[at, chip],
                preferred_element_type=jnp.float32,
            )
            if lane == 0:
                sums[at][here, :] = product
            else:
                sums[at][here, :] += product

    def near_multiply(at):
        weights[at].arrived(3)
        multiply(at, 1)
        weights[at].arrived(4)
        multiply(at, 2)

    def far_multiply(at):
        weights[at].arrived(7, 8)
        multiply(at, 3)

    loads[2].wait()
    fetch.wait()
    query.arrived(2)
    multiply(0, 0)
    key.arrived(2)
    multiply(1, 0)
    query.near()
    near_multiply(0)
    key.near()
    value.start(2, 0, 1)
    near_multiply(1)
    value.arrived(2)
    multiply(2, 0)
    query.far()
    far_multiply(0)
    key.far()
    far_multiply(1)
    for at in range(2):
        lin = sums[at][...]
        parts[peers.me, at] = lax.dot_general(
            jnp.ones((8, lin.shape[1]), jnp.float32),
            lin * lin,
            (((1,), (1,)), ((), ())),
            precision=lax.Precision.HIGHEST,
            preferred_element_type=jnp.float32,
        )
    peers.start()
    value.near()
    near_multiply(2)
    value.far()
    far_multiply(2)
    value_ref[...] = value_sum[...].astype(value_ref.dtype)
    peers.finish()
    squares_ref[...] = sum(parts[group] for group in range(peers.count))
    peers.sent()
    for weight in weights:
        weight.sent()


def project(tokens, query_weight, key_weight, value_weight, stride):
    count = tokens.shape[0]
    rows, width = query_weight.shape
    groups = lax.axis_size("head")
    anywhere = pl.BlockSpec(memory_space=pl.ANY)
    vmem = pl.BlockSpec(memory_space=pltpu.VMEM)
    return pl.pallas_call(
        functools.partial(project_kernel, stride),
        out_shape=(
            jax.ShapeDtypeStruct((count, width), jnp.float32),
            jax.ShapeDtypeStruct((count, width), jnp.float32),
            jax.ShapeDtypeStruct((count, width), jnp.bfloat16),
            jax.ShapeDtypeStruct((2, 8, count), jnp.float32),
        ),
        in_specs=[anywhere] * 4,
        out_specs=(vmem, vmem, vmem, vmem),
        scratch_shapes=[
            pltpu.VMEM(tokens.shape, tokens.dtype),
            pltpu.VMEM((3, CUBE // 2, 2 * rows, width), query_weight.dtype),
            pltpu.VMEM((count, width), jnp.float32),
            pltpu.VMEM((groups, 2, 8, count), jnp.float32),
            pltpu.SemaphoreType.DMA((4,)),
            pltpu.SemaphoreType.DMA((3, 9)),
            pltpu.SemaphoreType.DMA((3, 9)),
            pltpu.SemaphoreType.DMA((groups - 1,)),
            pltpu.SemaphoreType.DMA((groups - 1,)),
        ],
        compiler_params=pltpu.CompilerParams(
            collective_id=0, has_side_effects=True, vmem_limit_bytes=60 * 1024 * 1024
        ),
        name="project",
    )(tokens, query_weight, key_weight, value_weight)


class Line:
    def __init__(self, blocks, send, receive):
        self.count = lax.axis_size("head")
        self.me = lax.axis_index("head")
        self.blocks, self.send, self.receive = blocks, send, receive

    def neighbour(self, side):
        return self.me + 1 if side == 0 else self.me - 1

    def has(self, side):
        return self.me < self.count - 1 if side == 0 else self.me > 0

    def greet(self, semaphore):
        for side in range(2):
            @pl.when(self.has(side))
            def _():
                pl.semaphore_signal(
                    semaphore,
                    inc=1,
                    device_id={"head": self.neighbour(side)},
                    device_id_type=pl.DeviceIdType.MESH,
                )

    def number(self):
        return ones(self.me, self.count)

    def origin(self, side, far):
        return self.me - far if side == 0 else self.me + far

    def holds(self, side, far):
        return self.me >= far if side == 0 else self.me + far < self.count

    def copy(self, side, far, at, group):
        ref = self.blocks(group, at)
        return pltpu.make_async_remote_copy(
            src_ref=ref,
            dst_ref=ref,
            send_sem=self.send.at[side, far, at],
            recv_sem=self.receive.at[side, far, at],
            device_id={"head": self.neighbour(side)},
            device_id_type=pl.DeviceIdType.MESH,
        )

    def start(self, side, far, at):
        @pl.when(self.has(side) & self.holds(side, far))
        def _():
            self.copy(side, far, at, self.origin(side, far)).start()

    def relay(self, far, at):
        for side in range(2):
            @pl.when(self.holds(side, far + 1))
            def _():
                self.copy(side, far, at, self.origin(side, far + 1)).wait_recv()

            if far + 2 < self.count:
                self.start(side, far + 1, at)

    def sent(self, parts):
        for side in range(2):
            for far in range(self.count - 1):
                @pl.when(self.has(side) & self.holds(side, far))
                def _():
                    @pl.loop(0, parts)
                    def _(at):
                        self.copy(side, far, at, self.origin(side, far)).wait_send()


def ones(me, count):
    return 1 - lax.div(me + 1, count) + lax.div(me + count - 1, count)


class Halo:
    def __init__(self, sources, pads, grid_columns, side, local, send, receive, side_send, side_receive):
        place = lax.axis_index("hw")
        self.row, self.column = lax.div(place, grid_columns), lax.rem(place, grid_columns)
        self.place, self.columns = place, grid_columns
        self.sources, self.pads = sources, pads
        self.edge, self.body = WT * side, side * side
        self.slots = min(3, grid_columns)
        self.own = self.column if grid_columns == 2 else self.slots // 2
        self.local, self.send, self.receive = local, send, receive
        self.side_send, self.side_receive = side_send, side_receive
        self.parts = [
            pl.ds(self.edge, self.body),
            pl.ds(0, self.edge),
            pl.ds(self.edge + self.body, self.edge),
        ]

    def first_column(self):
        return 0 if self.columns == 2 else self.column - self.slots // 2

    def has(self, way):
        return [
            self.row > 0,
            self.row < DEV_ROWS - 1,
            self.column > 0,
            self.column < self.columns - 1,
        ][way]

    def device(self, way):
        step = [-self.columns, self.columns, -1, 1][way]
        return {"hw": self.place + step}

    def greet(self, semaphore):
        for way in range(4):
            @pl.when(self.has(way))
            def _():
                pl.semaphore_signal(
                    semaphore,
                    inc=1,
                    device_id=self.device(way),
                    device_id_type=pl.DeviceIdType.MESH,
                )

    def number(self):
        return ones(self.row, DEV_ROWS) + ones(self.column, self.columns)

    def vertical(self, kind, way):
        low = 0 if way == 0 else self.body - self.edge
        return pltpu.make_async_remote_copy(
            src_ref=self.sources[kind].at[:, pl.ds(low, self.edge), :],
            dst_ref=self.pads[kind].at[self.own, :, self.parts[2 - way], :],
            send_sem=self.send.at[kind, way],
            recv_sem=self.receive.at[kind, way],
            device_id=self.device(way),
            device_id_type=pl.DeviceIdType.MESH,
        )

    def sideways(self, kind, way, part):
        own = self.pads[kind].at[self.own, :, self.parts[part], :]
        if self.columns == 2:
            slot = self.own
        else:
            slot = self.slots - 1 if way == 2 else 0
        return pltpu.make_async_remote_copy(
            src_ref=self.sources[kind] if part == 0 else own,
            dst_ref=self.pads[kind].at[slot, :, self.parts[part], :],
            send_sem=self.side_send.at[kind, way - 2, part],
            recv_sem=self.side_receive.at[kind, way - 2, part],
            device_id=self.device(way),
            device_id_type=pl.DeviceIdType.MESH,
        )

    def here(self, kind):
        return pltpu.make_async_copy(
            self.sources[kind],
            self.pads[kind].at[self.own, :, self.parts[0], :],
            self.local.at[kind],
        )

    def start(self):
        for kind in range(2):
            self.here(kind).start()
        for kind in range(2):
            for way in range(2):
                @pl.when(self.has(way))
                def _():
                    self.vertical(kind, way).start()
            for way in (2, 3):
                @pl.when(self.has(way))
                def _():
                    self.sideways(kind, way, 0).start()
        for pad in self.pads:
            for way in range(2):
                @pl.when(jnp.logical_not(self.has(way)))
                def _():
                    for slot in range(self.slots):
                        place = pad.at[slot, :, self.parts[1 + way], :]
                        place[...] = jnp.zeros(place.shape, pad.dtype)

            if self.columns > 2:
                for way in (2, 3):
                    @pl.when(jnp.logical_not(self.has(way)))
                    def _():
                        place = pad.at[0 if way == 2 else self.slots - 1]
                        place[...] = jnp.zeros(place.shape, pad.dtype)

    def finish(self):
        for kind in range(2):
            for came in range(2):
                @pl.when(self.has(came))
                def _():
                    self.vertical(kind, 1 - came).wait_recv()
                    for way in (2, 3):
                        @pl.when(self.has(way))
                        def _():
                            self.sideways(kind, way, 1 + came).start()
        for kind in range(2):
            self.here(kind).wait()
            for came in (2, 3):
                @pl.when(self.has(came))
                def _():
                    self.sideways(kind, 5 - came, 0).wait_recv()
                    for part in range(2):
                        @pl.when(self.has(part))
                        def _():
                            self.sideways(kind, 5 - came, 1 + part).wait_recv()

    def sent(self):
        for kind in range(2):
            for way in range(2):
                @pl.when(self.has(way))
                def _():
                    self.vertical(kind, way).wait_send()
            for way in (2, 3):
                @pl.when(self.has(way))
                def _():
                    self.sideways(kind, way, 0).wait_send()
                    for part in range(2):
                        @pl.when(self.has(part))
                        def _():
                            self.sideways(kind, way, 1 + part).wait_send()


def weigh(scores, allowed):
    scores = jnp.where(allowed, scores, -jnp.inf)
    raised = jnp.exp(scores - jnp.max(scores, axis=-1, keepdims=True))
    return (raised * (1.0 / jnp.sum(raised, axis=-1, keepdims=True))).astype(jnp.bfloat16)


def score(queries, keys):
    return lax.dot_general(
        queries, keys, (((1,), (1,)), ((), ())), preferred_element_type=jnp.float32
    ) * (1.0 / math.sqrt(HD))


def attend_kernel(
    stride, grid_columns, frames, side,
    query_ref, key_ref, value_ref, output_hbm,
    result_ref,
    key_pad, value_pad, spatial, mixed, held, total, local, send, receive, line_send, line_receive,
    halo_local, halo_send, halo_receive, side_send, side_receive,
):
    cube = Cube(stride)
    rows, columns = output_hbm.shape
    weight = Exchange(cube, held, send, receive, rows)
    load = pltpu.make_async_copy(output_hbm, weight.own, local)
    load.start()
    group_width = query_ref.shape[1]
    heads_here = group_width // HD
    tokens = query_ref.shape[0]

    def head_of(at):
        return pl.ds(pl.multiple_of(at * HD, HD), HD)

    line = Line(lambda group, at: mixed.at[group, :, head_of(at)], line_send, line_receive)
    halo = Halo(
        (key_ref, value_ref), (key_pad, value_pad), grid_columns, side,
        halo_local, halo_send, halo_receive, side_send, side_receive,
    )
    cube.barrier((line, halo))
    halo.start()
    load.wait()

    area = side * side
    tall = side + 2 * WT
    window = tall * side
    keys_here = halo.slots * window
    tiles = side // WT
    query_at = lax.broadcasted_iota(jnp.int32, (area, keys_here), 0)
    key_at = lax.broadcasted_iota(jnp.int32, (area, keys_here), 1)
    key_row = halo.row * tiles - 1 + key_at % window // side // WT
    key_column = (halo.first_column() + key_at // window) * tiles + key_at % side // WT
    down = key_row - halo.row * tiles - query_at // side // WT
    right = key_column - halo.column * tiles - query_at % side // WT
    near = (down >= -1) & (down <= 1) & (right >= -1) & (right <= 1)
    near &= (key_row >= 0) & (key_row < DEV_ROWS * tiles)
    near &= (key_column >= 0) & (key_column < grid_columns * tiles)
    strip = 2 * area
    same = (
        lax.broadcasted_iota(jnp.int32, (strip, tokens), 0) % area
        == lax.broadcasted_iota(jnp.int32, (strip, tokens), 1) % area
    )

    halo.finish()
    weight.start(2, 0, 1)

    def window_of(pad, frame, head):
        return jnp.concatenate([pad[slot, frame, :, head] for slot in range(halo.slots)], axis=0)

    @pl.loop(0, heads_here)
    def _(at):
        head = head_of(at)
        own_keys = key_ref[:, :, head].reshape(tokens, HD)
        scores = [
            score(query_ref[pl.ds(frame * area, area), head], window_of(key_pad, frame, head))
            for frame in range(frames)
        ]
        weights = [weigh(one, near) for one in scores]
        for frame in range(frames):
            spatial[pl.ds(frame * area, area), :] = jnp.dot(
                weights[frame], window_of(value_pad, frame, head), preferred_element_type=jnp.float32
            ).astype(jnp.bfloat16)
        for low in range(0, tokens, strip):
            over = weigh(score(query_ref[pl.ds(low, strip), head], own_keys), same)
            mixed[line.me, pl.ds(low, strip), head] = jnp.dot(
                over, spatial[...], preferred_element_type=jnp.float32
            ).astype(jnp.bfloat16)
        line.start(0, 0, at)
        line.start(1, 0, at)

    block = tokens // 2

    def multiply(group, first=False):
        @pl.loop(0, 2)
        def _(step):
            here = pl.ds(pl.multiple_of(step * block, block), block)
            product = jnp.dot(mixed[group, here, :], held[group], preferred_element_type=jnp.float32)
            if first:
                total[here, :] = product
            else:
                total[here, :] += product

    def relay(far):
        @pl.loop(0, heads_here)
        def _(at):
            line.relay(far, at)

    relay(0)
    weight.near()
    weight.arrived(2, 3, 4)
    if line.count > 2:
        relay(1)
    weight.far()
    weight.arrived(7, 8)
    multiply(line.me, True)
    for far in range(line.count - 1):
        if far > 1:
            relay(far)
        for side_at in range(2):
            @pl.when(line.holds(side_at, far + 1))
            def _():
                multiply(line.origin(side_at, far + 1))
    result_ref[...] = total[...].astype(result_ref.dtype)
    weight.sent()
    line.sent(heads_here)
    halo.sent()


def attend(queries, keys, values, output_weight, stride, grid_columns, frames, side):
    tokens, group_width = queries.shape
    rows, columns = output_weight.shape
    groups = lax.axis_size("head")
    pad = pltpu.VMEM(
        (min(3, grid_columns), frames, side * (side + 2 * WT), group_width), jnp.bfloat16
    )
    heads_here = group_width // HD
    vmem = pl.BlockSpec(memory_space=pltpu.VMEM)
    return pl.pallas_call(
        functools.partial(attend_kernel, stride, grid_columns, frames, side),
        out_shape=jax.ShapeDtypeStruct((tokens, columns), jnp.bfloat16),
        in_specs=[vmem] * 3 + [pl.BlockSpec(memory_space=pl.ANY)],
        out_specs=vmem,
        scratch_shapes=[
            pad,
            pad,
            pltpu.VMEM((tokens, HD), jnp.bfloat16),
            pltpu.VMEM((groups, tokens, group_width), jnp.bfloat16),
            pltpu.VMEM((CUBE // 2, 2 * rows, columns), output_weight.dtype),
            pltpu.VMEM((tokens, columns), jnp.float32),
            pltpu.SemaphoreType.DMA,
            pltpu.SemaphoreType.DMA((9,)),
            pltpu.SemaphoreType.DMA((9,)),
            pltpu.SemaphoreType.DMA((2, groups - 1, heads_here)),
            pltpu.SemaphoreType.DMA((2, groups - 1, heads_here)),
            pltpu.SemaphoreType.DMA((2,)),
            pltpu.SemaphoreType.DMA((2, 2)),
            pltpu.SemaphoreType.DMA((2, 2)),
            pltpu.SemaphoreType.DMA((2, 2, 3)),
            pltpu.SemaphoreType.DMA((2, 2, 3)),
        ],
        compiler_params=pltpu.CompilerParams(
            collective_id=1, has_side_effects=True, vmem_limit_bytes=60 * 1024 * 1024
        ),
        name="attend",
    )(queries, keys, values, output_weight)


def pregather(weight, stride):
    if stride == 1:
        return weight
    count = lax.axis_size("hw")
    groups = [list(range(first, first + stride)) for first in range(0, count, stride)]
    return lax.all_gather(weight, "hw", axis=0, tiled=True, axis_index_groups=groups)


def per_device(
    latents,
    query_weight,
    key_weight,
    value_weight,
    output_weight,
    query_gain,
    key_gain,
    frame_index,
    row_index,
    column_index,
):
    frames, side, width = (latents.shape[1], latents.shape[2], latents.shape[4])
    tokens = latents.reshape(frames * side * side, width)
    head_dim = HD
    full_width = HEADS * HD
    group_width = query_weight.shape[1]
    heads_here = group_width // head_dim
    grid_columns = lax.axis_size("hw") // DEV_ROWS
    place = lax.axis_index("hw")
    grid_row = place // grid_columns
    grid_column = place % grid_columns
    stride = lax.axis_size("hw") // CUBE
    query_lin, key_lin, values, squares = project(
        tokens,
        *(pregather(w, stride) for w in (query_weight, key_weight, value_weight)),
        stride,
    )
    query_squares, key_squares = squares[0, 0], squares[1, 0]
    query_norm = query_lin * lax.rsqrt(query_squares / full_width + NORM_EPS)[:, None] * query_gain
    key_norm = key_lin * lax.rsqrt(key_squares / full_width + NORM_EPS)[:, None] * key_gain
    rows_here = lax.dynamic_slice_in_dim(row_index, grid_row * side, side)
    columns_here = lax.dynamic_slice_in_dim(column_index, grid_column * side, side)
    angle = rope_angles(frame_index, rows_here, columns_here, head_dim)
    cosine, sine = jnp.cos(angle), jnp.sin(angle)
    queries = rotate(query_norm, cosine, sine, heads_here, head_dim)
    keys = rotate(key_norm, cosine, sine, heads_here, head_dim)
    result = attend(
        queries,
        keys.reshape(frames, -1, group_width),
        values.reshape(frames, -1, group_width),
        pregather(output_weight, stride),
        stride,
        grid_columns,
        frames,
        side,
    )
    return result.reshape(1, frames, side, side, output_weight.shape[1])


def solution(mesh):
    placed = (
        P("hw", None, None, None, None),
        P("hw", "head"),
        P("hw", "head"),
        P("hw", "head"),
        P("hw", "head"),
        P("head"),
        P("head"),
        P(),
        P(),
        P(),
    )
    return jax.shard_map(
        per_device,
        mesh=mesh,
        in_specs=placed,
        out_specs=P("hw", None, None, None, "head"),
        check_vma=False,
    )
```

profile of v0, /device:TPU:4, one launch (start us, length us, event | category | flops | bytes accessed | tf_op | source)
XLA Modules:
  0.0 189.5 jit_solution(799688787486551747)
XLA Ops:
  0.0 0.7 dynamic-slice_convert_fusion
  0.7 0.7 dynamic-slice_convert_fusion.1
  1.5 0.7 convert_element_type.45
  2.1 0.1 fusion.44
  2.2 0.1 broadcast_in_dim.7
  2.3 0.2 mul.165
  2.5 0.1 broadcast_in_dim.6
  2.5 0.1 mul.160
  2.7 0.1 broadcast_multiply_fusion.1
  2.8 0.1 broadcast_in_dim.8
  2.8 0.1 mul.170
  3.0 0.1 broadcast_multiply_fusion
  3.1 0.9 add_cosine_fusion
  4.0 0.0 copy-start.2
  4.0 0.0 copy-start.3
  4.0 89.1 %project.1 = (f32[512,640]{1,0:T(8,128)}, f32[512,640]{1,0:T(8,128)}, bf16[512,640]{1,0:T(8,128)(2,1)}, f32[2,8,512]{2,1,0:T(8,128)}) custom-call(bf16[512,5120]{1,0:T(8,128)(2,1)} %bitcast.29, bf16[640,640]{1,0:T(8,128)(2,1)} %query_hbm.1, bf16[640,640]{1,0:T(8,128)(2,1)} %key_hbm.1, bf16[640,640]{1,0:T(8,128)(2,1)} %value_hbm.1), custom_call_target="tpu_custom_call" | custom-call | tf_op jit(solution)/shard_map/project/pallas_call | solution.py:293
  93.1 0.7 add_rsqrt_fusion
  93.9 0.0 copy-done.2
  93.9 0.0 copy-done.3
  93.9 2.0 %multiply_multiply_fusion = (f32[512,640]{1,0:T(8,128)S(1)}, f32[512,640]{1,0:T(8,128)S(1)}) fusion(f32[512,640]{1,0:T(8,128)} %get-tuple-element.11, f32[640]{0:T(1024)S(1)} %copy-done.2, f32[512]{0:T(512)S(1)} %bitcast.32, f32[640]{0:T(1024)S(1)} %copy-done.3, f32[512,640]{1,0:T(8,128)} %get-tuple-element.9, f32[512]{0:T(512)S(1)} %bitcast.33), kind=kLoop, calls=%fused_computation | loop fusion | flops 1310720 | bytes 5252096 | tf_op jit(solution)/shard_map/mul | solution.py:737
  95.9 0.4 fusion.41
  96.3 0.4 fusion.40
  96.7 0.4 fusion.5
  97.1 0.4 fusion.1
  97.5 0.4 fusion.43
  97.9 0.4 fusion.42
  98.3 0.4 fusion.9
  98.7 0.4 fusion.15
  99.0 0.4 fusion.11
  99.6 0.0 copy-start
  99.8 0.6 copy-done
  100.4 0.0 copy-start.1
  100.4 0.8 copy-done.1
  101.3 85.7 %attend.1 = bf16[512,1280]{1,0:T(8,128)(2,1)} custom-call(bf16[512,640]{1,0:T(8,128)(2,1)} %copy-done.1, bf16[8,64,640]{2,1,0:T(8,128)(2,1)} %bitcast.30, bf16[8,64,640]{2,1,0:T(8,128)(2,1)} %bitcast.31, bf16[320,1280]{1,0:T(8,128)(2,1)} %output_hbm.1), custom_call_target="tpu_custom_call" | custom-call | tf_op jit(solution)/shard_map/attend/pallas_call | solution.py:669
  187.0 2.5 %copy.20 = bf16[1,8,8,8,1280]{4,3,2,1,0:T(8,128)(2,1)} copy(bf16[1,8,8,8,1280]{4,3,2,1,0:T(8,128)(2,1)} %bitcast.28) | data formatting | bytes 2621440
  (16 shorter events, 0.4 us)
Async XLA Ops:
  4.0 89.9 %copy-start.2 = (f32[640]{0:T(1024)S(1)}, f32[640]{0:T(1024)}, u32[]{:S(2)}) copy-start(f32[640]{0:T(1024)} %param.16) | copy-start | bytes 7684
  4.0 89.9 %copy-start.3 = (f32[640]{0:T(1024)S(1)}, f32[640]{0:T(1024)}, u32[]{:S(2)}) copy-start(f32[640]{0:T(1024)} %param.15) | copy-start | bytes 7684
  99.6 0.8 copy-start
  100.4 0.8 copy-start.1
where the time goes:
time: 190 us; the launch traced here: 189 us
  Pallas kernels  175 us (92%)
  other arithmetic  7.73 us (4%)
  local copies, waits for them, and re-layouts  6.68 us (4%)
    pallas_call x1, Pallas kernels, project(): pl.pallas_call(functools.partial(project_kernel, stride), out_shape=(jax....  89.1 us
    pallas_call x1, Pallas kernels, attend(): pl.pallas_call(functools.partial(attend_kernel, stride, grid_columns, fra...  85.7 us
    unnamed x17, local copies, waits for them, and re-layouts  4.2 us

commit v1 on v0

v1 whole, which is shorter than its diff:
```python
import functools
import math

import jax
import jax.numpy as jnp
import numpy as np
from jax import lax
from jax.experimental import pallas as pl
from jax.experimental.pallas import tpu as pltpu
from jax.sharding import PartitionSpec as P

HEADS = 20
HD = 128
WT = 4
DEV_ROWS = 4


NORM_EPS = 0.5


def lane_tables(head_dim):
    side_pairs = head_dim // 6
    frame_pairs = head_dim // 2 - 2 * side_pairs

    def lanes(before, count, after):
        table = np.power(10000.0, -np.arange(count) / count)
        return np.repeat(np.pad(table, (before, after)), 2)

    tables = np.zeros((8, head_dim), np.float32)
    tables[0] = lanes(0, frame_pairs, 2 * side_pairs)
    tables[1] = lanes(frame_pairs, side_pairs, side_pairs)
    tables[2] = lanes(frame_pairs + side_pairs, side_pairs, 0)
    return tables


CUBE = 8


class Cube:
    def __init__(self, stride):
        me = lax.axis_index("hw")
        within = lax.rem(me, stride) if stride > 1 else 0
        place = lax.div(me, stride) if stride > 1 else me
        core = lax.rem(place, 2)
        x = lax.rem(lax.div(place, 2), 2)
        y = lax.div(place, 4)
        self.place = place
        self.other = [place + 1 - 2 * core, place + 2 - 4 * x, place + 4 - 8 * y]
        self.diagonal = place + 2 - 4 * x + 4 - 8 * y
        self.devices = [{"hw": other * stride + within} for other in self.other]
        self.chip = lax.div(place, 2)
        self.chips = [
            self.chip,
            self.chip + 1 - 2 * x,
            self.chip + 2 - 4 * y,
            self.chip + 3 - 2 * x - 4 * y,
        ]

    def barrier(self, line):
        semaphore = pltpu.get_barrier_semaphore()
        for peers in line:
            peers.greet(semaphore)
        for device in self.devices:
            pl.semaphore_signal(semaphore, inc=1, device_id=device, device_id_type=pl.DeviceIdType.MESH)
        count = sum((peers.number() for peers in line), len(self.devices))
        pl.semaphore_wait(semaphore, count)


class Exchange:
    def __init__(self, cube, held, send, receive, rows, lanes=None):
        core_place, x_place, y_place = cube.other
        half = rows * SPLIT // 10 // 16 * 16

        def part(place, low, size):
            start = pl.multiple_of(lax.rem(place, 2) * rows + low, 16)
            if lanes is None:
                return held.at[lax.div(place, 2), pl.ds(start, size)]
            return held.at[lax.div(place, 2), pl.ds(start, size), lanes]

        def copy(at, place, low, size, partner):
            ref = part(place, low, size)
            return pltpu.make_async_remote_copy(
                src_ref=ref,
                dst_ref=ref,
                send_sem=send.at[at],
                recv_sem=receive.at[at],
                device_id=cube.devices[partner],
                device_id_type=pl.DeviceIdType.MESH,
            )

        rest = rows - half
        self.own = part(cube.place, 0, rows)
        moves = [
            (cube.place, 0, rows, 1),
            (cube.place, 0, rows, 2),
            (cube.place, 0, rows, 0),
            (x_place, 0, rows, 0),
            (y_place, 0, rows, 0),
            (x_place, 0, half, 2),
            (y_place, half, rest, 1),
            (cube.diagonal, 0, half, 0),
            (cube.diagonal, half, rest, 0),
        ]
        self.copy = lambda at: copy(at, *moves[at])

    def start(self, *which):
        for at in which:
            self.copy(at).start()

    def begin(self):
        self.start(0, 1, 2)

    def arrived(self, *which):
        for at in which:
            self.copy(at).wait_recv()

    def near(self):
        self.arrived(0)
        self.start(5, 3)
        self.arrived(1)
        self.start(6, 4)

    def far(self):
        self.arrived(5)
        self.start(7)
        self.arrived(6)
        self.start(8)

    def sent(self):
        for at in range(9):
            self.copy(at).wait_send()


class Peers:
    def __init__(self, parts, send, receive):
        self.count = lax.axis_size("head")
        self.me = lax.axis_index("head")
        self.parts, self.send, self.receive = parts, send, receive

    def device(self, step):
        return {"head": lax.rem(self.me + step, self.count)}

    def greet(self, semaphore):
        for step in range(1, self.count):
            pl.semaphore_signal(
                semaphore,
                inc=1,
                device_id=self.device(step),
                device_id_type=pl.DeviceIdType.MESH,
            )

    def number(self):
        return self.count - 1

    def copy(self, at, step, group):
        ref = self.parts.at[group, at]
        return pltpu.make_async_remote_copy(
            src_ref=ref,
            dst_ref=ref,
            send_sem=self.send.at[at, step - 1],
            recv_sem=self.receive.at[at, step - 1],
            device_id=self.device(step),
            device_id_type=pl.DeviceIdType.MESH,
        )

    def start(self, at):
        for step in range(1, self.count):
            self.copy(at, step, self.me).start()

    def finish(self, at):
        for step in range(1, self.count):
            self.copy(at, step, lax.rem(self.me + self.count - step, self.count)).wait_recv()

    def sent(self, at):
        for step in range(1, self.count):
            self.copy(at, step, self.me).wait_send()


class Line:
    def __init__(self, blocks, send, receive):
        self.count = lax.axis_size("head")
        self.me = lax.axis_index("head")
        self.blocks, self.send, self.receive = blocks, send, receive

    def neighbour(self, side):
        return self.me + 1 if side == 0 else self.me - 1

    def has(self, side):
        return self.me < self.count - 1 if side == 0 else self.me > 0

    def origin(self, side, far):
        return self.me - far if side == 0 else self.me + far

    def holds(self, side, far):
        return self.me >= far if side == 0 else self.me + far < self.count

    def copy(self, side, far, at, group):
        ref = self.blocks(group, at)
        return pltpu.make_async_remote_copy(
            src_ref=ref,
            dst_ref=ref,
            send_sem=self.send.at[side, far, at],
            recv_sem=self.receive.at[side, far, at],
            device_id={"head": self.neighbour(side)},
            device_id_type=pl.DeviceIdType.MESH,
        )

    def start(self, side, far, at):
        @pl.when(self.has(side) & self.holds(side, far))
        def _():
            self.copy(side, far, at, self.origin(side, far)).start()

    def relay(self, far, at):
        for side in range(2):
            @pl.when(self.holds(side, far + 1))
            def _():
                self.copy(side, far, at, self.origin(side, far + 1)).wait_recv()

            if far + 2 < self.count:
                self.start(side, far + 1, at)

    def sent(self, parts):
        for side in range(2):
            for far in range(self.count - 1):
                @pl.when(self.has(side) & self.holds(side, far))
                def _():
                    @pl.loop(0, parts)
                    def _(at):
                        self.copy(side, far, at, self.origin(side, far)).wait_send()


def ones(me, count):
    return 1 - lax.div(me + 1, count) + lax.div(me + count - 1, count)


class Grid:
    def __init__(self, grid_columns, side):
        place = lax.axis_index("hw")
        self.row, self.column = lax.div(place, grid_columns), lax.rem(place, grid_columns)
        self.place, self.columns = place, grid_columns
        self.edge, self.body = WT * side, side * side
        self.slots = min(3, grid_columns)
        self.own = self.column if grid_columns == 2 else self.slots // 2
        self.parts = [
            pl.ds(self.edge, self.body),
            pl.ds(0, self.edge),
            pl.ds(self.edge + self.body, self.edge),
        ]

    def first_column(self):
        return 0 if self.columns == 2 else self.column - self.slots // 2

    def has(self, way):
        return [
            self.row > 0,
            self.row < DEV_ROWS - 1,
            self.column > 0,
            self.column < self.columns - 1,
        ][way]

    def device(self, way):
        step = [-self.columns, self.columns, -1, 1][way]
        return {"hw": self.place + step}

    def greet(self, semaphore):
        for way in range(4):
            @pl.when(self.has(way))
            def _():
                pl.semaphore_signal(
                    semaphore,
                    inc=1,
                    device_id=self.device(way),
                    device_id_type=pl.DeviceIdType.MESH,
                )

    def number(self):
        return ones(self.row, DEV_ROWS) + ones(self.column, self.columns)

    def clear(self, pad):
        for way in range(2):
            @pl.when(jnp.logical_not(self.has(way)))
            def _():
                for slot in range(self.slots):
                    place = pad.at[slot, :, self.parts[1 + way], :]
                    place[...] = jnp.zeros(place.shape, pad.dtype)

        if self.columns > 2:
            for way in (2, 3):
                @pl.when(jnp.logical_not(self.has(way)))
                def _():
                    place = pad.at[0 if way == 2 else self.slots - 1]
                    place[...] = jnp.zeros(place.shape, pad.dtype)


class Halo:
    def __init__(self, grid, pad, lanes, sems):
        self.grid, self.pad, self.lanes = grid, pad, lanes
        self.send, self.receive, self.side_send, self.side_receive = sems

    def at(self, slot, pixels):
        return self.pad.at[slot, :, pixels, self.lanes]

    def vertical(self, way):
        grid = self.grid
        low = grid.edge if way == 0 else grid.body
        return pltpu.make_async_remote_copy(
            src_ref=self.at(grid.own, pl.ds(low, grid.edge)),
            dst_ref=self.at(grid.own, grid.parts[2 - way]),
            send_sem=self.send.at[way],
            recv_sem=self.receive.at[way],
            device_id=grid.device(way),
            device_id_type=pl.DeviceIdType.MESH,
        )

    def sideways(self, way, part):
        grid = self.grid
        if grid.columns == 2:
            slot = grid.own
        else:
            slot = grid.slots - 1 if way == 2 else 0
        return pltpu.make_async_remote_copy(
            src_ref=self.at(grid.own, grid.parts[part]),
            dst_ref=self.at(slot, grid.parts[part]),
            send_sem=self.side_send.at[way - 2, part],
            recv_sem=self.side_receive.at[way - 2, part],
            device_id=grid.device(way),
            device_id_type=pl.DeviceIdType.MESH,
        )

    def start(self):
        for way in range(2):
            @pl.when(self.grid.has(way))
            def _():
                self.vertical(way).start()
        for way in (2, 3):
            @pl.when(self.grid.has(way))
            def _():
                self.sideways(way, 0).start()

    def relay(self):
        for came in range(2):
            @pl.when(self.grid.has(came))
            def _():
                self.vertical(1 - came).wait_recv()
                for way in (2, 3):
                    @pl.when(self.grid.has(way))
                    def _():
                        self.sideways(way, 1 + came).start()

    def finish(self):
        for came in (2, 3):
            @pl.when(self.grid.has(came))
            def _():
                self.sideways(5 - came, 0).wait_recv()
                for part in range(2):
                    @pl.when(self.grid.has(part))
                    def _():
                        self.sideways(5 - came, 1 + part).wait_recv()

    def sent(self):
        for way in range(2):
            @pl.when(self.grid.has(way))
            def _():
                self.vertical(way).wait_send()
        for way in (2, 3):
            @pl.when(self.grid.has(way))
            def _():
                self.sideways(way, 0).wait_send()
                for part in range(2):
                    @pl.when(self.grid.has(part))
                    def _():
                        self.sideways(way, 1 + part).wait_send()


def weigh(scores, allowed):
    scores = jnp.where(allowed, scores, -jnp.inf)
    raised = jnp.exp(scores - jnp.max(scores, axis=-1, keepdims=True))
    return (raised * (1.0 / jnp.sum(raised, axis=-1, keepdims=True))).astype(jnp.bfloat16)


def score(queries, keys):
    return lax.dot_general(
        queries, keys, (((1,), (1,)), ((), ())), preferred_element_type=jnp.float32
    ) * (1.0 / math.sqrt(HD))


SPLIT = 6
STRIP = 16
KEY, QUERY = 0, 1


def block_kernel(
    stride, grid_columns, frames, side,
    tokens_hbm, query_hbm, key_hbm, value_hbm, output_hbm,
    query_gain, key_gain, lanes_ref, frame_index, row_index, column_index,
    result_ref,
    tokens, held, held_value, held_output, sums, trig, query_ref, key_pad, value_pad,
    temporal, spatial, picked, mixed, parts,
    local, send, receive, value_send, value_receive, output_send, output_receive,
    parts_send, parts_receive, line_send, line_receive,
    halo_send, halo_receive, side_send, side_receive,
):
    cube = Cube(stride)
    rows, group_width = query_hbm.shape
    depth = 2 * rows
    output_rows, columns = output_hbm.shape
    heads_here = group_width // HD
    slab = columns // heads_here
    count = tokens.shape[0]
    area = side * side
    block = count // 2

    def head_of(at):
        return pl.ds(pl.multiple_of(at * HD, HD), HD)

    weights = [Exchange(cube, held.at[at], send.at[at], receive.at[at], rows) for at in range(2)]

    def value(at):
        return Exchange(
            cube, held_value, value_send.at[at], value_receive.at[at], rows, head_of(at)
        )

    def slab_of(at):
        return pl.ds(pl.multiple_of(at * slab, 128), slab)

    def output(at):
        return Exchange(
            cube, held_output, output_send.at[at], output_receive.at[at], output_rows, slab_of(at)
        )

    mine = lax.rem(cube.place, 2)
    loads = [
        pltpu.make_async_copy(key_hbm, weights[KEY].own, local.at[0]),
        pltpu.make_async_copy(query_hbm, weights[QUERY].own, local.at[1]),
        pltpu.make_async_copy(tokens_hbm, tokens, local.at[2]),
        pltpu.make_async_copy(
            value_hbm,
            held_value.at[cube.chip, pl.ds(pl.multiple_of(mine * rows, 16), rows)],
            local.at[3],
        ),
        pltpu.make_async_copy(
            output_hbm,
            held_output.at[cube.chip, pl.ds(pl.multiple_of(mine * output_rows, 16), output_rows)],
            local.at[4],
        ),
    ]
    for load in loads:
        load.start()

    peers = Peers(parts, parts_send, parts_receive)
    line = Line(lambda group, at: mixed.at[group, :, :, head_of(at)], line_send, line_receive)
    grid = Grid(grid_columns, side)

    def halo(pad, lanes, at):
        return Halo(
            grid, pad, lanes,
            (halo_send.at[at], halo_receive.at[at], side_send.at[at], side_receive.at[at]),
        )

    key_halo = halo(key_pad, pl.ds(0, group_width), heads_here)

    def value_halo(at):
        return halo(value_pad, head_of(at), at)

    cube.barrier((peers, grid))
    key, query = weights[KEY], weights[QUERY]
    loads[0].wait()
    key.begin()
    loads[1].wait()
    query.begin()

    grid.clear(key_pad)
    grid.clear(value_pad)
    pixel = lax.broadcasted_iota(jnp.int32, (side, HD), 0)
    across = jnp.zeros((side, HD), jnp.float32)
    for at in range(side):
        here = column_index[grid.column * side + at].astype(jnp.float32)
        across = jnp.where(pixel == at, here, across)
    across = across * lanes_ref[2:3, :]

    @pl.loop(0, frames)
    def _(frame):
        along = frame_index[frame].astype(jnp.float32) * lanes_ref[0:1, :]
        for at in range(side):
            down = row_index[grid.row * side + at].astype(jnp.float32) * lanes_ref[1:2, :]
            angle = along + down + across
            here = pl.ds(pl.multiple_of(frame * area + at * side, 8), side)
            trig[0, here, :] = jnp.cos(angle)
            trig[1, here, :] = jnp.sin(angle)

    def multiply(at, lane):
        chip = cube.chips[lane]

        @pl.loop(0, 2)
        def _(step):
            here = pl.ds(pl.multiple_of(step * block, block), block)
            product = jnp.dot(
                tokens[here, pl.ds(pl.multiple_of(chip * depth, 128), depth)],
                held[at, chip],
                preferred_element_type=jnp.float32,
            )
            if lane == 0:
                sums[at, here, :] = product
            else:
                sums[at, here, :] += product

    def near_multiply(at):
        weights[at].arrived(3)
        multiply(at, 1)
        weights[at].arrived(4)
        multiply(at, 2)

    def far_multiply(at):
        weights[at].arrived(7, 8)
        multiply(at, 3)

    def squares(at):
        lin = sums[at]
        parts[peers.me, at] = lax.dot_general(
            jnp.ones((8, group_width), jnp.float32),
            lin * lin,
            (((1,), (1,)), ((), ())),
            precision=lax.Precision.HIGHEST,
            preferred_element_type=jnp.float32,
        )
        peers.start(at)

    span = HD // area
    even = lax.broadcasted_iota(jnp.int32, (HD, HD), 1) % 2 == 0

    def rotate(at, gain, store):
        peers.finish(at)

        @pl.loop(0, count // HD)
        def _(step):
            here = pl.ds(pl.multiple_of(step * HD, HD), HD)
            total = sum(parts[group, at, :, here] for group in range(peers.count))
            scale = lax.rsqrt(total / (HEADS * HD) + NORM_EPS)
            scale = jnp.broadcast_to(scale[0:1, :], (HD, HD)).T
            cosine, sine = trig[0, here, :], trig[1, here, :]
            for head in range(heads_here):
                lanes = slice(head * HD, (head + 1) * HD)
                one = sums[at, here, lanes] * scale * gain[0:1, lanes]
                turned = jnp.where(even, -jnp.roll(one, -1, axis=1), jnp.roll(one, 1, axis=1))
                turned = (one * cosine + turned * sine).astype(jnp.bfloat16)
                store(pl.ds(step * span, span), lanes, turned.reshape(span, area, HD))

    def store_key(where, lanes, block_values):
        key_pad[grid.own, where, grid.parts[0], lanes] = block_values

    def store_query(where, lanes, block_values):
        query_ref[where, :, lanes] = block_values

    loads[2].wait()
    key.arrived(2)
    multiply(KEY, 0)
    query.arrived(2)
    multiply(QUERY, 0)
    key.near()
    near_multiply(KEY)
    loads[3].wait()
    loads[4].wait()
    query.near()
    value(0).begin()
    near_multiply(QUERY)
    key.far()
    far_multiply(KEY)
    squares(KEY)
    rotate(KEY, key_gain, store_key)
    key_halo.start()
    value(1).begin()
    query.far()
    far_multiply(QUERY)
    squares(QUERY)
    value(0).near()
    key_halo.relay()
    rotate(QUERY, query_gain, store_query)

    same = (
        lax.broadcasted_iota(jnp.int32, (frames * STRIP, frames * STRIP), 0) % STRIP
        == lax.broadcasted_iota(jnp.int32, (frames * STRIP, frames * STRIP), 1) % STRIP
    )

    @pl.loop(0, heads_here)
    def _(at):
        head = head_of(at)
        for low in range(0, area, STRIP):
            scores = score(
                query_ref[:, pl.ds(low, STRIP), head].reshape(frames * STRIP, HD),
                key_pad[grid.own, :, pl.ds(grid.edge + low, STRIP), head].reshape(frames * STRIP, HD),
            )
            temporal[at, low // STRIP] = weigh(scores, same)

    tall = side + 2 * WT
    window = tall * side
    keys_here = grid.slots * window
    tiles = side // WT
    query_at = lax.broadcasted_iota(jnp.int32, (area, keys_here), 0)
    key_at = lax.broadcasted_iota(jnp.int32, (area, keys_here), 1)
    key_row = grid.row * tiles - 1 + key_at % window // side // WT
    key_column = (grid.first_column() + key_at // window) * tiles + key_at % side // WT
    down = key_row - grid.row * tiles - query_at // side // WT
    right = key_column - grid.column * tiles - query_at % side // WT
    close = (down >= -1) & (down <= 1) & (right >= -1) & (right <= 1)
    close &= (key_row >= 0) & (key_row < DEV_ROWS * tiles)
    close &= (key_column >= 0) & (key_column < grid_columns * tiles)

    def window_of(pad, frame, head):
        return jnp.concatenate([pad[slot, frame, :, head] for slot in range(grid.slots)], axis=0)

    key_halo.finish()

    @pl.loop(0, heads_here)
    def _(at):
        head = head_of(at)
        for frame in range(frames):
            scores = score(query_ref[frame, :, head], window_of(key_pad, frame, head))
            spatial[at, frame] = weigh(scores, close)

    def begin(at):
        @pl.when(at < heads_here)
        def _():
            value(at).begin()

        @pl.when((at >= heads_here) & (at < 2 * heads_here))
        def _():
            output(at - heads_here).begin()

    def near(at):
        @pl.when(at < heads_here)
        def _():
            value(at).near()

        @pl.when((at >= heads_here) & (at < 2 * heads_here))
        def _():
            output(at - heads_here).near()

    def relays(at):
        for far in range(line.count - 1):
            from_head = at - 1 - far

            @pl.when((from_head >= 0) & (from_head < heads_here))
            def _():
                line.relay(far, from_head)

    half_frames = frames // 2

    @pl.loop(0, heads_here)
    def _(at):
        head = head_of(at)
        weight = value(at)
        weight.far()
        begin(at + 2)
        weight.arrived(2, 3, 4, 7, 8)

        @pl.loop(0, 2)
        def _(step):
            here = pl.ds(pl.multiple_of(step * block, block), block)
            product = sum(
                jnp.dot(
                    tokens[here, chip * depth : (chip + 1) * depth],
                    held_value[chip, :, head],
                    preferred_element_type=jnp.float32,
                )
                for chip in range(CUBE // 2)
            )
            value_pad[grid.own, pl.ds(step * half_frames, half_frames), grid.parts[0], head] = (
                product.astype(jnp.bfloat16).reshape(half_frames, area, HD)
            )

        border = value_halo(at)
        border.start()
        near(at + 1)
        relays(at)
        border.relay()
        border.finish()
        for frame in range(frames):
            picked[frame] = jnp.dot(
                spatial[at, frame],
                window_of(value_pad, frame, head),
                preferred_element_type=jnp.float32,
            ).astype(jnp.bfloat16)
        for low in range(0, area, STRIP):
            mixed[line.me, :, pl.ds(low, STRIP), head] = (
                jnp.dot(
                    temporal[at, low // STRIP],
                    picked[:, pl.ds(low, STRIP), :].reshape(frames * STRIP, HD),
                    preferred_element_type=jnp.float32,
                )
                .astype(jnp.bfloat16)
                .reshape(frames, STRIP, HD)
            )
        line.start(0, 0, at)
        line.start(1, 0, at)

    def project(at):
        @pl.loop(0, 2)
        def _(step):
            total = sum(
                jnp.dot(
                    mixed[group, pl.ds(step * half_frames, half_frames)].reshape(block, group_width),
                    held_output[group, :, slab_of(at)],
                    preferred_element_type=jnp.float32,
                )
                for group in range(line.count)
            )
            here = pl.ds(pl.multiple_of(step * block, block), block)
            result_ref[here, slab_of(at)] = total.astype(result_ref.dtype)

    whole_at = line.count - 2

    @pl.loop(0, heads_here)
    def _(at):
        weight = output(at)
        weight.far()
        begin(heads_here + at + 2)
        near(heads_here + at + 1)
        relays(heads_here + at)
        weight.arrived(2, 3, 4, 7, 8)

        @pl.when(at == whole_at)
        def _():
            @pl.loop(0, whole_at + 1)
            def _(one):
                project(one)

        @pl.when(at > whole_at)
        def _():
            project(at)

    for weight in weights:
        weight.sent()
    for at in range(2):
        peers.sent(at)
    key_halo.sent()

    @pl.loop(0, heads_here)
    def _(at):
        value(at).sent()
        output(at).sent()
        value_halo(at).sent()

    line.sent(heads_here)


def attention_block(
    tokens, query_weight, key_weight, value_weight, output_weight,
    query_gain, key_gain, frame_index, row_index, column_index, stride, grid_columns, frames, side,
):
    count = tokens.shape[0]
    rows, width = query_weight.shape
    output_rows, columns = output_weight.shape
    groups = lax.axis_size("head")
    heads_here = width // HD
    slots = min(3, grid_columns)
    area = side * side
    tall = side * (side + 2 * WT)
    anywhere = pl.BlockSpec(memory_space=pl.ANY)
    vmem = pl.BlockSpec(memory_space=pltpu.VMEM)
    smem = pl.BlockSpec(memory_space=pltpu.SMEM)
    pad = pltpu.VMEM((slots, frames, tall, width), jnp.bfloat16)
    dma = pltpu.SemaphoreType.DMA
    strip = frames * STRIP
    return pl.pallas_call(
        functools.partial(block_kernel, stride, grid_columns, frames, side),
        out_shape=jax.ShapeDtypeStruct((count, columns), jnp.bfloat16),
        in_specs=[anywhere] * 5 + [vmem] * 3 + [smem] * 3,
        out_specs=vmem,
        scratch_shapes=[
            pltpu.VMEM(tokens.shape, tokens.dtype),
            pltpu.VMEM((2, CUBE // 2, 2 * rows, width), query_weight.dtype),
            pltpu.VMEM((CUBE // 2, 2 * rows, width), value_weight.dtype),
            pltpu.VMEM((CUBE // 2, 2 * output_rows, columns), output_weight.dtype),
            pltpu.VMEM((2, count, width), jnp.float32),
            pltpu.VMEM((2, count, HD), jnp.float32),
            pltpu.VMEM((frames, area, width), jnp.bfloat16),
            pad,
            pad,
            pltpu.VMEM((heads_here, area // STRIP, strip, strip), jnp.bfloat16),
            pltpu.VMEM((heads_here, frames, area, slots * tall), jnp.bfloat16),
            pltpu.VMEM((frames, area, HD), jnp.bfloat16),
            pltpu.VMEM((groups, frames, area, width), jnp.bfloat16),
            pltpu.VMEM((groups, 2, 8, count), jnp.float32),
            dma((5,)),
            dma((2, 9)),
            dma((2, 9)),
            dma((heads_here, 9)),
            dma((heads_here, 9)),
            dma((heads_here, 9)),
            dma((heads_here, 9)),
            dma((2, groups - 1)),
            dma((2, groups - 1)),
            dma((2, groups - 1, heads_here)),
            dma((2, groups - 1, heads_here)),
            dma((heads_here + 1, 2)),
            dma((heads_here + 1, 2)),
            dma((heads_here + 1, 2, 3)),
            dma((heads_here + 1, 2, 3)),
        ],
        compiler_params=pltpu.CompilerParams(
            collective_id=0, has_side_effects=True, vmem_limit_bytes=60 * 1024 * 1024
        ),
        name="attention_block",
    )(
        tokens, query_weight, key_weight, value_weight, output_weight,
        query_gain[None], key_gain[None], jnp.asarray(lane_tables(HD)),
        frame_index, row_index, column_index,
    )


def pregather(weight, stride):
    if stride == 1:
        return weight
    count = lax.axis_size("hw")
    groups = [list(range(first, first + stride)) for first in range(0, count, stride)]
    return lax.all_gather(weight, "hw", axis=0, tiled=True, axis_index_groups=groups)


def per_device(
    latents,
    query_weight,
    key_weight,
    value_weight,
    output_weight,
    query_gain,
    key_gain,
    frame_index,
    row_index,
    column_index,
):
    frames, side, width = (latents.shape[1], latents.shape[2], latents.shape[4])
    tokens = latents.reshape(frames * side * side, width)
    grid_columns = lax.axis_size("hw") // DEV_ROWS
    stride = lax.axis_size("hw") // CUBE
    result = attention_block(
        tokens,
        *(pregather(w, stride) for w in (query_weight, key_weight, value_weight, output_weight)),
        query_gain, key_gain, frame_index, row_index, column_index,
        stride, grid_columns, frames, side,
    )
    return result.reshape(1, frames, side, side, output_weight.shape[1])


def solution(mesh):
    placed = (
        P("hw", None, None, None, None),
        P("hw", "head"),
        P("hw", "head"),
        P("hw", "head"),
        P("hw", "head"),
        P("head"),
        P("head"),
        P(),
        P(),
        P(),
    )
    return jax.shard_map(
        per_device,
        mesh=mesh,
        in_specs=placed,
        out_specs=P("hw", None, None, None, "head"),
        check_vma=False,
    )
```

time: 190 us -> 172 us (0.905); the launches traced: 189 us -> 169 us
  Pallas kernels: 175 us -> 164 us
  other arithmetic: 7.73 us -> 0 us
    pallas_call x2 -> x1, Pallas kernels: 175 us -> 164 us  [attention_block(): pl.pallas_call(functools.partial(block_kernel, stride, grid_columns, fram...]
    convert_element_type x8 -> x0, other arithmetic: 3.89 us -> none  [the longest x5 1.77 us: rotate(): heads.append((one * cosine + turned * sine).astype(jnp.bfloat16))]
    broadcast_in_dim x3 -> x2, local copies, waits for them, and re-layouts: 0.21 us -> 2.53 us  [the longest x1 1.27 us: attention_block(): query_gain[None]]
    mul x3 -> x0, other arithmetic: 2.14 us -> none  [the longest x1 1.99 us: per_device(): key_lin * lax.rsqrt(key_squares / full_width + NORM_EPS)[:, None] * key_gain]
    unnamed x17 -> x1, local copies, waits for them, and re-layouts: 4.2 us -> 2.47 us
where the time goes in v1:
time: 172 us; the launch traced here: 169 us
  Pallas kernels  164 us (95%)
  local copies, waits for them, and re-layouts  5 us (3%)
    pallas_call x1, Pallas kernels, attention_block(): pl.pallas_call(functools.partial(block_kernel, stride, grid_columns, fram...  164 us

profile of v1, /device:TPU:4, one launch (start us, length us, event | category | flops | bytes accessed | tf_op | source)
XLA Modules:
  0.0 169.0 jit_solution(2298527840458696000)
XLA Ops:
  0.0 1.3 broadcast_in_dim.6.query_gain
  1.3 1.3 broadcast_in_dim.7.key_gain
  2.5 164.0 %attention_block.1 = bf16[512,1280]{1,0:T(8,128)(2,1)} custom-call(bf16[512,5120]{1,0:T(8,128)(2,1)} %bitcast.3, bf16[640,640]{1,0:T(8,128)(2,1)} %query_hbm.1, bf16[640,640]{1,0:T(8,128)(2,1)} %key_hbm.1, bf16[640,640]{1,0:T(8,128)(2,1)} %value_hbm.1, bf16[320,1280]{1,0:T(8,128)(2,1)} %output_hbm.1, f32[1,640]{1,0:T(1,128)} %broadcast_in_dim.6.query_gain, ...), custom_call_target="tpu_custom_call" | custom-call | tf_op jit(solution)/shard_map/attention_block/pallas_call | solution.py:764
  166.5 2.5 %copy.13 = bf16[1,8,8,8,1280]{4,3,2,1,0:T(8,128)(2,1)} copy(bf16[1,8,8,8,1280]{4,3,2,1,0:T(8,128)(2,1)} %bitcast.2) | data formatting | bytes 2621440

commit v2 on v1

--- a/solution.py
+++ b/solution.py
@@ -67,9 +67,9 @@
 
 
 class Exchange:
-    def __init__(self, cube, held, send, receive, rows, lanes=None):
+    def __init__(self, cube, held, send, receive, rows, tenths, lanes=None):
         core_place, x_place, y_place = cube.other
-        half = rows * SPLIT // 10 // 16 * 16
+        half = rows * tenths // 10 // 16 * 16
 
         def part(place, low, size):
             start = pl.multiple_of(lax.rem(place, 2) * rows + low, 16)
@@ -328,10 +328,16 @@
         )
 
     def start(self):
+        self.start_vertical()
+        self.start_sideways()
+
+    def start_vertical(self):
         for way in range(2):
             @pl.when(self.grid.has(way))
             def _():
                 self.vertical(way).start()
+
+    def start_sideways(self):
         for way in (2, 3):
             @pl.when(self.grid.has(way))
             def _():
@@ -384,7 +390,8 @@
     ) * (1.0 / math.sqrt(HD))
 
 
-SPLIT = 6
+SPLIT = 7
+DEPTH = 3
 STRIP = 16
 KEY, QUERY = 0, 1
 
@@ -393,10 +400,10 @@
     stride, grid_columns, frames, side,
     tokens_hbm, query_hbm, key_hbm, value_hbm, output_hbm,
     query_gain, key_gain, lanes_ref, frame_index, row_index, column_index,
-    result_ref,
-    tokens, held, held_value, held_output, sums, trig, query_ref, key_pad, value_pad,
+    result_hbm,
+    result_ref, tokens, held, held_value, held_output, sums, trig, query_ref, key_pad, value_pad,
     temporal, spatial, picked, mixed, parts,
-    local, send, receive, value_send, value_receive, output_send, output_receive,
+    local, store, send, receive, value_send, value_receive, output_send, output_receive,
     parts_send, parts_receive, line_send, line_receive,
     halo_send, halo_receive, side_send, side_receive,
 ):
@@ -413,11 +420,11 @@
     def head_of(at):
         return pl.ds(pl.multiple_of(at * HD, HD), HD)
 
-    weights = [Exchange(cube, held.at[at], send.at[at], receive.at[at], rows) for at in range(2)]
+    weights = [Exchange(cube, held.at[at], send.at[at], receive.at[at], rows, 5) for at in range(2)]
 
     def value(at):
         return Exchange(
-            cube, held_value, value_send.at[at], value_receive.at[at], rows, head_of(at)
+            cube, held_value, value_send.at[at], value_receive.at[at], rows, SPLIT, head_of(at)
         )
 
     def slab_of(at):
@@ -425,7 +432,7 @@
 
     def output(at):
         return Exchange(
-            cube, held_output, output_send.at[at], output_receive.at[at], output_rows, slab_of(at)
+            cube, held_output, output_send.at[at], output_receive.at[at], output_rows, SPLIT, slab_of(at)
         )
 
     mine = lax.rem(cube.place, 2)
@@ -444,8 +451,8 @@
             local.at[4],
         ),
     ]
-    for load in loads:
-        load.start()
+    for at in (3, 0, 1, 2, 4):
+        loads[at].start()
 
     peers = Peers(parts, parts_send, parts_receive)
     line = Line(lambda group, at: mixed.at[group, :, :, head_of(at)], line_send, line_receive)
@@ -462,15 +469,19 @@
     def value_halo(at):
         return halo(value_pad, head_of(at), at)
 
-    cube.barrier((peers, grid))
+    with jax.named_scope("barrier"):
+        cube.barrier((peers, grid))
     key, query = weights[KEY], weights[QUERY]
+    loads[3].wait()
+    value(0).begin()
     loads[0].wait()
     key.begin()
     loads[1].wait()
     query.begin()
 
-    grid.clear(key_pad)
-    grid.clear(value_pad)
+    with jax.named_scope("clear"):
+        grid.clear(key_pad)
+        grid.clear(value_pad)
     pixel = lax.broadcasted_iota(jnp.int32, (side, HD), 0)
     across = jnp.zeros((side, HD), jnp.float32)
     for at in range(side):
@@ -479,6 +490,7 @@
     across = across * lanes_ref[2:3, :]
 
     @pl.loop(0, frames)
+    @jax.named_scope("trig")
     def _(frame):
         along = frame_index[frame].astype(jnp.float32) * lanes_ref[0:1, :]
         for at in range(side):
@@ -529,8 +541,6 @@
     even = lax.broadcasted_iota(jnp.int32, (HD, HD), 1) % 2 == 0
 
     def rotate(at, gain, store):
-        peers.finish(at)
-
         @pl.loop(0, count // HD)
         def _(step):
             here = pl.ds(pl.multiple_of(step * HD, HD), HD)
@@ -540,7 +550,7 @@
             cosine, sine = trig[0, here, :], trig[1, here, :]
             for head in range(heads_here):
                 lanes = slice(head * HD, (head + 1) * HD)
-                one = sums[at, here, lanes] * scale * gain[0:1, lanes]
+                one = sums[at, here, lanes] * scale * gain[lanes].reshape(1, HD)
                 turned = jnp.where(even, -jnp.roll(one, -1, axis=1), jnp.roll(one, 1, axis=1))
                 turned = (one * cosine + turned * sine).astype(jnp.bfloat16)
                 store(pl.ds(step * span, span), lanes, turned.reshape(span, area, HD))
@@ -550,46 +560,11 @@
 
     def store_query(where, lanes, block_values):
         query_ref[where, :, lanes] = block_values
-
-    loads[2].wait()
-    key.arrived(2)
-    multiply(KEY, 0)
-    query.arrived(2)
-    multiply(QUERY, 0)
-    key.near()
-    near_multiply(KEY)
-    loads[3].wait()
-    loads[4].wait()
-    query.near()
-    value(0).begin()
-    near_multiply(QUERY)
-    key.far()
-    far_multiply(KEY)
-    squares(KEY)
-    rotate(KEY, key_gain, store_key)
-    key_halo.start()
-    value(1).begin()
-    query.far()
-    far_multiply(QUERY)
-    squares(QUERY)
-    value(0).near()
-    key_halo.relay()
-    rotate(QUERY, query_gain, store_query)
 
     same = (
         lax.broadcasted_iota(jnp.int32, (frames * STRIP, frames * STRIP), 0) % STRIP
         == lax.broadcasted_iota(jnp.int32, (frames * STRIP, frames * STRIP), 1) % STRIP
     )
-
-    @pl.loop(0, heads_here)
-    def _(at):
-        head = head_of(at)
-        for low in range(0, area, STRIP):
-            scores = score(
-                query_ref[:, pl.ds(low, STRIP), head].reshape(frames * STRIP, HD),
-                key_pad[grid.own, :, pl.ds(grid.edge + low, STRIP), head].reshape(frames * STRIP, HD),
-            )
-            temporal[at, low // STRIP] = weigh(scores, same)
 
     tall = side + 2 * WT
     window = tall * side
@@ -608,52 +583,16 @@
     def window_of(pad, frame, head):
         return jnp.concatenate([pad[slot, frame, :, head] for slot in range(grid.slots)], axis=0)
 
-    key_halo.finish()
-
-    @pl.loop(0, heads_here)
-    def _(at):
+    mark = jax.named_scope
+    half_frames = frames // 2
+
+    def multiply_value(at):
         head = head_of(at)
-        for frame in range(frames):
-            scores = score(query_ref[frame, :, head], window_of(key_pad, frame, head))
-            spatial[at, frame] = weigh(scores, close)
-
-    def begin(at):
-        @pl.when(at < heads_here)
-        def _():
-            value(at).begin()
-
-        @pl.when((at >= heads_here) & (at < 2 * heads_here))
-        def _():
-            output(at - heads_here).begin()
-
-    def near(at):
-        @pl.when(at < heads_here)
-        def _():
-            value(at).near()
-
-        @pl.when((at >= heads_here) & (at < 2 * heads_here))
-        def _():
-            output(at - heads_here).near()
-
-    def relays(at):
-        for far in range(line.count - 1):
-            from_head = at - 1 - far
-
-            @pl.when((from_head >= 0) & (from_head < heads_here))
-            def _():
-                line.relay(far, from_head)
-
-    half_frames = frames // 2
-
-    @pl.loop(0, heads_here)
-    def _(at):
-        head = head_of(at)
-        weight = value(at)
-        weight.far()
-        begin(at + 2)
-        weight.arrived(2, 3, 4, 7, 8)
+        with mark("v_arrived"):
+            value(at).arrived(2, 3, 4, 7, 8)
 
         @pl.loop(0, 2)
+        @jax.named_scope("v_multiply")
         def _(step):
             here = pl.ds(pl.multiple_of(step * block, block), block)
             product = sum(
@@ -668,33 +607,193 @@
                 product.astype(jnp.bfloat16).reshape(half_frames, area, HD)
             )
 
-        border = value_halo(at)
-        border.start()
-        near(at + 1)
-        relays(at)
-        border.relay()
-        border.finish()
+        value_halo(at).start()
+
+    with mark("tokens_wait"):
+        loads[2].wait()
+    with mark("k0_wait"):
+        key.arrived(2)
+    with mark("k0"):
+        multiply(KEY, 0)
+    with mark("q0_wait"):
+        query.arrived(2)
+    with mark("q0"):
+        multiply(QUERY, 0)
+    with mark("v_near0"):
+        value(0).near()
+    with mark("k_near"):
+        key.near()
+    with mark("k12"):
+        near_multiply(KEY)
+    loads[4].wait()
+    with mark("q_near"):
+        query.near()
+    with mark("q12"):
+        near_multiply(QUERY)
+    with mark("v_far"):
+        value(0).far()
+    multiply_value(0)
+    value(1).begin()
+    with mark("k_far"):
+        key.far()
+    with mark("k3"):
+        far_multiply(KEY)
+    with mark("k_squares"):
+        squares(KEY)
+    with mark("k_peers"):
+        peers.finish(KEY)
+    with mark("k_rotate"):
+        rotate(KEY, key_gain, store_key)
+    key_halo.start_vertical()
+    with mark("q_far"):
+        query.far()
+    key_halo.start_sideways()
+    with mark("q3"):
+        far_multiply(QUERY)
+    with mark("q_squares"):
+        squares(QUERY)
+    with mark("v_halo0"):
+        value_halo(0).relay()
+    with mark("v_near1"):
+        value(1).near()
+    value(2).begin()
+    with mark("q_peers"):
+        peers.finish(QUERY)
+    with mark("q_rotate"):
+        rotate(QUERY, query_gain, store_query)
+    with mark("k_halo_relay"):
+        key_halo.relay()
+
+    @jax.named_scope("weights")
+    def make_weights(at):
+        head = head_of(at)
+        for low in range(0, area, STRIP):
+            scores = score(
+                query_ref[:, pl.ds(low, STRIP), head].reshape(frames * STRIP, HD),
+                key_pad[grid.own, :, pl.ds(grid.edge + low, STRIP), head].reshape(frames * STRIP, HD),
+            )
+            temporal[low // STRIP] = weigh(scores, same)
+        for frame in range(frames):
+            scores = score(query_ref[frame, :, head], window_of(key_pad, frame, head))
+            spatial[frame] = weigh(scores, close)
+
+    @jax.named_scope("attend")
+    def attend(at):
+        head = head_of(at)
         for frame in range(frames):
             picked[frame] = jnp.dot(
-                spatial[at, frame],
+                spatial[frame],
                 window_of(value_pad, frame, head),
                 preferred_element_type=jnp.float32,
             ).astype(jnp.bfloat16)
         for low in range(0, area, STRIP):
             mixed[line.me, :, pl.ds(low, STRIP), head] = (
                 jnp.dot(
-                    temporal[at, low // STRIP],
+                    temporal[low // STRIP],
                     picked[:, pl.ds(low, STRIP), :].reshape(frames * STRIP, HD),
                     preferred_element_type=jnp.float32,
                 )
                 .astype(jnp.bfloat16)
                 .reshape(frames, STRIP, HD)
             )
+
+    def relays(at):
+        for far in range(line.count - 1):
+            from_head = at - 2 - far
+
+            @pl.when((from_head >= 1) & (from_head < heads_here))
+            def _():
+                line.relay(far, from_head)
+
+    def share(at):
+        with mark("v_halo_finish"):
+            value_halo(at).finish()
+        attend(at)
         line.start(0, 0, at)
         line.start(1, 0, at)
 
+    with mark("k_halo_finish"):
+        key_halo.finish()
+    make_weights(0)
+    share(0)
+    with mark("early_sent"):
+        for weight in weights:
+            weight.sent()
+        for at in range(2):
+            peers.sent(at)
+        key_halo.sent()
+    value(3).begin()
+    with mark("line0"):
+        line.relay(0, 0)
+
+    @pl.loop(1, heads_here + 1)
+    def _(at):
+        @pl.when(at < heads_here - 1)
+        @jax.named_scope("v_near")
+        def _():
+            value(at + 1).near()
+
+        @pl.when(at >= heads_here - 1)
+        @jax.named_scope("v_near")
+        def _():
+            output(at + 1 - heads_here).near()
+
+        @pl.when(at < heads_here)
+        @jax.named_scope("v_far")
+        def _():
+            value(at).far()
+
+        @pl.when(at == heads_here)
+        @jax.named_scope("v_far")
+        def _():
+            output(0).far()
+
+        @pl.when(at > 1)
+        def _():
+            make_weights(at - 1)
+            with mark("v_halo_relay"):
+                value_halo(at - 1).relay()
+
+        @pl.when(at < heads_here)
+        def _():
+            multiply_value(at)
+
+        @pl.when(at < heads_here - DEPTH)
+        def _():
+            value(at + DEPTH).begin()
+
+        @pl.when((at >= heads_here - DEPTH) & (at < heads_here - 1))
+        def _():
+            output(at + DEPTH - heads_here).begin()
+
+        @pl.when(at == heads_here - 1)
+        def _():
+            @pl.loop(DEPTH - 1, heads_here)
+            def _(one):
+                output(one).begin()
+
+        @pl.when(at > 1)
+        def _():
+            share(at - 1)
+
+        for far in range(1, line.count - 1):
+            @pl.when(at == far)
+            @jax.named_scope("line0")
+            def _():
+                line.relay(far, 0)
+
+        with mark("v_line_relays"):
+            relays(at)
+
+
+    def stored(at):
+        return pltpu.make_async_copy(
+            result_ref.at[:, slab_of(at)], result_hbm.at[:, slab_of(at)], store.at[at]
+        )
+
     def project(at):
         @pl.loop(0, 2)
+        @jax.named_scope("project")
         def _(step):
             total = sum(
                 jnp.dot(
@@ -707,16 +806,32 @@
             here = pl.ds(pl.multiple_of(step * block, block), block)
             result_ref[here, slab_of(at)] = total.astype(result_ref.dtype)
 
-    whole_at = line.count - 2
+        stored(at).start()
+
+    whole_at = 2
 
     @pl.loop(0, heads_here)
     def _(at):
-        weight = output(at)
-        weight.far()
-        begin(heads_here + at + 2)
-        near(heads_here + at + 1)
-        relays(heads_here + at)
-        weight.arrived(2, 3, 4, 7, 8)
+        @pl.when(at < heads_here - 2)
+        @jax.named_scope("o_near")
+        def _():
+            output(at + 2).near()
+
+        @pl.when(at < heads_here - 1)
+        @jax.named_scope("o_far")
+        def _():
+            output(at + 1).far()
+
+        @pl.when(at <= whole_at)
+        @jax.named_scope("o_line_relays")
+        def _():
+            relays(heads_here + 1 + at)
+
+        with mark("v_sent"):
+            value(at).sent()
+            value_halo(at).sent()
+        with mark("o_arrived"):
+            output(at).arrived(2, 3, 4, 7, 8)
 
         @pl.when(at == whole_at)
         def _():
@@ -728,19 +843,16 @@
         def _():
             project(at)
 
-    for weight in weights:
-        weight.sent()
-    for at in range(2):
-        peers.sent(at)
-    key_halo.sent()
-
-    @pl.loop(0, heads_here)
-    def _(at):
-        value(at).sent()
-        output(at).sent()
-        value_halo(at).sent()
-
-    line.sent(heads_here)
+    with mark("sent"):
+        @pl.loop(0, heads_here)
+        def _(at):
+            output(at).sent()
+
+        line.sent(heads_here)
+
+        @pl.loop(0, heads_here)
+        def _(at):
+            stored(at).wait()
 
 
 def attention_block(
@@ -765,8 +877,9 @@
         functools.partial(block_kernel, stride, grid_columns, frames, side),
         out_shape=jax.ShapeDtypeStruct((count, columns), jnp.bfloat16),
         in_specs=[anywhere] * 5 + [vmem] * 3 + [smem] * 3,
-        out_specs=vmem,
+        out_specs=anywhere,
         scratch_shapes=[
+            pltpu.VMEM((count, columns), jnp.bfloat16),
             pltpu.VMEM(tokens.shape, tokens.dtype),
             pltpu.VMEM((2, CUBE // 2, 2 * rows, width), query_weight.dtype),
             pltpu.VMEM((CUBE // 2, 2 * rows, width), value_weight.dtype),
@@ -776,12 +889,13 @@
             pltpu.VMEM((frames, area, width), jnp.bfloat16),
             pad,
             pad,
-            pltpu.VMEM((heads_here, area // STRIP, strip, strip), jnp.bfloat16),
-            pltpu.VMEM((heads_here, frames, area, slots * tall), jnp.bfloat16),
+            pltpu.VMEM((area // STRIP, strip, strip), jnp.bfloat16),
+            pltpu.VMEM((frames, area, slots * tall), jnp.bfloat16),
             pltpu.VMEM((frames, area, HD), jnp.bfloat16),
             pltpu.VMEM((groups, frames, area, width), jnp.bfloat16),
             pltpu.VMEM((groups, 2, 8, count), jnp.float32),
             dma((5,)),
+            dma((heads_here,)),
             dma((2, 9)),
             dma((2, 9)),
             dma((heads_here, 9)),
@@ -803,7 +917,7 @@
         name="attention_block",
     )(
         tokens, query_weight, key_weight, value_weight, output_weight,
-        query_gain[None], key_gain[None], jnp.asarray(lane_tables(HD)),
+        query_gain, key_gain, jnp.asarray(lane_tables(HD)),
         frame_index, row_index, column_index,
     )
 

time: 172 us -> 156 us (0.907); the launches traced: 169 us -> 155 us
  Pallas kernels: 164 us -> 153 us
  local copies, waits for them, and re-layouts: 5 us -> 2.47 us
    pallas_call x1, Pallas kernels: 164 us -> 153 us  [attention_block(): pl.pallas_call(functools.partial(block_kernel, stride, grid_columns, fram...]
    broadcast_in_dim x2 -> x0, local copies, waits for them, and re-layouts: 2.53 us -> none  [the longest x1 1.27 us: attention_block(): query_gain[None]]
where the time goes in v2:
time: 156 us; the launch traced here: 155 us
  Pallas kernels  153 us (98%)
  local copies, waits for them, and re-layouts  2.47 us (2%)
    pallas_call x1, Pallas kernels, attention_block(): pl.pallas_call(functools.partial(block_kernel, stride, grid_columns, fram...  153 us

profile of v2, /device:TPU:4, one launch (start us, length us, event | category | flops | bytes accessed | tf_op | source)
XLA Modules:
  0.0 155.4 jit_solution(14720300469828107651)
XLA Ops:
  0.0 153.0 %attention_block.1 = bf16[512,1280]{1,0:T(8,128)(2,1)} custom-call(bf16[512,5120]{1,0:T(8,128)(2,1)} %bitcast.2, bf16[640,640]{1,0:T(8,128)(2,1)} %query_hbm.1, bf16[640,640]{1,0:T(8,128)(2,1)} %key_hbm.1, bf16[640,640]{1,0:T(8,128)(2,1)} %value_hbm.1, bf16[320,1280]{1,0:T(8,128)(2,1)} %output_hbm.1, f32[640]{0:T(1024)} %query_gain.1, f32[640]{0:T(1024)} %key_gain.1, ...), custom_call_target="tpu_custom_call" | custom-call | tf_op jit(solution)/shard_map/attention_block/pallas_call | solution.py:876
  153.0 2.5 %copy.13 = bf16[1,8,8,8,1280]{4,3,2,1,0:T(8,128)(2,1)} copy(bf16[1,8,8,8,1280]{4,3,2,1,0:T(8,128)(2,1)} %bitcast.3) | data formatting | bytes 2621440

commit v3 on v2

--- a/solution.py
+++ b/solution.py
@@ -68,6 +68,7 @@
 
 class Exchange:
     def __init__(self, cube, held, send, receive, rows, tenths, lanes=None):
+        arrivals = [0, 1, 2, 3, 4, 5, 6, 7, 8] if lanes is None else [0, 1, 2, 2, 2, 3, 4, 2, 2]
         core_place, x_place, y_place = cube.other
         half = rows * tenths // 10 // 16 * 16
 
@@ -82,8 +83,8 @@
             return pltpu.make_async_remote_copy(
                 src_ref=ref,
                 dst_ref=ref,
-                send_sem=send.at[at],
-                recv_sem=receive.at[at],
+                send_sem=send.at[0 if partner else 1],
+                recv_sem=receive.at[arrivals[at]],
                 device_id=cube.devices[partner],
                 device_id_type=pl.DeviceIdType.MESH,
             )
@@ -103,6 +104,22 @@
         ]
         self.copy = lambda at: copy(at, *moves[at])
 
+        def together(chips, size, sent_by, arrived_at):
+            ref = held.at[pl.ds(0, chips), pl.ds(0, size)]
+            if lanes is not None:
+                ref = held.at[pl.ds(0, chips), pl.ds(0, size), lanes]
+            return pltpu.make_async_remote_copy(
+                src_ref=ref,
+                dst_ref=ref,
+                send_sem=send.at[sent_by],
+                recv_sem=receive.at[arrived_at],
+                device_id=cube.devices[0],
+                device_id_type=pl.DeviceIdType.MESH,
+            )
+
+        self.links = lambda: together(3, rows, 0, 0)
+        self.within = lambda: together(2, 2 * rows, 1, 2)
+
     def start(self, *which):
         for at in which:
             self.copy(at).start()
@@ -126,9 +143,12 @@
         self.arrived(6)
         self.start(8)
 
+    def arrived_all(self):
+        self.within().wait_recv()
+
     def sent(self):
-        for at in range(9):
-            self.copy(at).wait_send()
+        self.links().wait_send()
+        self.within().wait_send()
 
 
 class Peers:
@@ -199,8 +219,8 @@
         return pltpu.make_async_remote_copy(
             src_ref=ref,
             dst_ref=ref,
-            send_sem=self.send.at[side, far, at],
-            recv_sem=self.receive.at[side, far, at],
+            send_sem=self.send.at[side, far],
+            recv_sem=self.receive.at[side, far, 0 if at is None else at],
             device_id={"head": self.neighbour(side)},
             device_id_type=pl.DeviceIdType.MESH,
         )
@@ -219,14 +239,12 @@
             if far + 2 < self.count:
                 self.start(side, far + 1, at)
 
-    def sent(self, parts):
+    def sent(self):
         for side in range(2):
             for far in range(self.count - 1):
                 @pl.when(self.has(side) & self.holds(side, far))
                 def _():
-                    @pl.loop(0, parts)
-                    def _(at):
-                        self.copy(side, far, at, self.origin(side, far)).wait_send()
+                    self.copy(side, far, None, self.origin(side, far)).wait_send()
 
 
 def ones(me, count):
@@ -293,24 +311,69 @@
 
 
 class Halo:
-    def __init__(self, grid, pad, lanes, sems):
-        self.grid, self.pad, self.lanes = grid, pad, lanes
-        self.send, self.receive, self.side_send, self.side_receive = sems
-
-    def at(self, slot, pixels):
-        return self.pad.at[slot, :, pixels, self.lanes]
+    def __init__(self, grid, pad, lanes, sems, stage=None):
+        self.grid, self.pad, self.lanes, self.stage = grid, pad, lanes, stage
+        self.send, self.receive, self.side_send, self.side_receive = sems[:4]
+        if stage is not None:
+            self.half_send, self.half_receive = sems[4:]
+        self.frames = pad.shape[1]
+        self.direct = pl.ds(0, self.frames if stage is None else self.frames // 2)
+        self.rest = pl.ds(self.frames // 2, self.frames // 2)
+
+    def at(self, slot, pixels, frames=None):
+        if frames is None:
+            frames = pl.ds(0, self.frames)
+        return self.pad.at[slot, frames, pixels, self.lanes]
+
+    def border(self, way):
+        grid = self.grid
+        return pl.ds(grid.edge if way == 0 else grid.body, grid.edge)
 
     def vertical(self, way):
         grid = self.grid
-        low = grid.edge if way == 0 else grid.body
         return pltpu.make_async_remote_copy(
-            src_ref=self.at(grid.own, pl.ds(low, grid.edge)),
-            dst_ref=self.at(grid.own, grid.parts[2 - way]),
+            src_ref=self.at(grid.own, self.border(way), self.direct),
+            dst_ref=self.at(grid.own, grid.parts[2 - way], self.direct),
             send_sem=self.send.at[way],
             recv_sem=self.receive.at[way],
             device_id=grid.device(way),
             device_id_type=pl.DeviceIdType.MESH,
         )
+
+    def second(self, way, move):
+        grid = self.grid
+        there = self.at(grid.own, grid.parts[2 - way], self.rest)
+        step = 1 if way == 1 else -1
+        distance = [step, 2 * step, -step][move]
+        return pltpu.make_async_remote_copy(
+            src_ref=self.stage if move == 2 else self.at(grid.own, self.border(way), self.rest),
+            dst_ref=self.stage if move == 1 else there,
+            send_sem=self.half_send.at[way, int(move == 2)],
+            recv_sem=self.half_receive.at[way, int(move == 1)],
+            device_id={"hw": grid.place + distance * grid.columns},
+            device_id_type=pl.DeviceIdType.MESH,
+        )
+
+    def start_second(self):
+        for way in range(2):
+            far = self.grid.row == 2 - way
+
+            @pl.when(far)
+            def _():
+                self.second(way, 1).start()
+
+            @pl.when(self.grid.has(way) & jnp.logical_not(far))
+            def _():
+                self.second(way, 0).start()
+
+    def forward(self):
+        if self.stage is None:
+            return
+        for way in range(2):
+            @pl.when(self.grid.row == (DEV_ROWS - 1) * way)
+            def _():
+                self.second(way, 1).wait_recv()
+                self.second(way, 2).start()
 
     def sideways(self, way, part):
         grid = self.grid
@@ -336,6 +399,8 @@
             @pl.when(self.grid.has(way))
             def _():
                 self.vertical(way).start()
+        if self.stage is not None:
+            self.start_second()
 
     def start_sideways(self):
         for way in (2, 3):
@@ -348,6 +413,8 @@
             @pl.when(self.grid.has(came))
             def _():
                 self.vertical(1 - came).wait_recv()
+                if self.stage is not None:
+                    self.second(1 - came, 0).wait_recv()
                 for way in (2, 3):
                     @pl.when(self.grid.has(way))
                     def _():
@@ -368,6 +435,13 @@
             @pl.when(self.grid.has(way))
             def _():
                 self.vertical(way).wait_send()
+                if self.stage is not None:
+                    self.second(way, 0).wait_send()
+
+            if self.stage is not None:
+                @pl.when(self.grid.row == (DEV_ROWS - 1) * way)
+                def _():
+                    self.second(way, 2).wait_send()
         for way in (2, 3):
             @pl.when(self.grid.has(way))
             def _():
@@ -401,11 +475,11 @@
     tokens_hbm, query_hbm, key_hbm, value_hbm, output_hbm,
     query_gain, key_gain, lanes_ref, frame_index, row_index, column_index,
     result_hbm,
-    result_ref, tokens, held, held_value, held_output, sums, trig, query_ref, key_pad, value_pad,
-    temporal, spatial, picked, mixed, parts,
+    result_ref, total, tokens, held, held_value, held_output, sums, trig, query_ref, key_pad, value_pad,
+    temporal, spatial, picked, mixed, parts, stage,
     local, store, send, receive, value_send, value_receive, output_send, output_receive,
     parts_send, parts_receive, line_send, line_receive,
-    halo_send, halo_receive, side_send, side_receive,
+    halo_send, halo_receive, side_send, side_receive, half_send, half_receive,
 ):
     cube = Cube(stride)
     rows, group_width = query_hbm.shape
@@ -455,7 +529,10 @@
         loads[at].start()
 
     peers = Peers(parts, parts_send, parts_receive)
-    line = Line(lambda group, at: mixed.at[group, :, :, head_of(at)], line_send, line_receive)
+    line = Line(
+        lambda group, at: mixed.at[group] if at is None else mixed.at[group, :, :, head_of(at)],
+        line_send, line_receive,
+    )
     grid = Grid(grid_columns, side)
 
     def halo(pad, lanes, at):
@@ -465,6 +542,16 @@
         )
 
     key_halo = halo(key_pad, pl.ds(0, group_width), heads_here)
+    if grid_columns == 2:
+        key_halo = Halo(
+            grid, key_pad, pl.ds(0, group_width),
+            (
+                halo_send.at[heads_here], halo_receive.at[heads_here],
+                side_send.at[heads_here], side_receive.at[heads_here],
+                half_send, half_receive,
+            ),
+            stage,
+        )
 
     def value_halo(at):
         return halo(value_pad, head_of(at), at)
@@ -544,8 +631,8 @@
         @pl.loop(0, count // HD)
         def _(step):
             here = pl.ds(pl.multiple_of(step * HD, HD), HD)
-            total = sum(parts[group, at, :, here] for group in range(peers.count))
-            scale = lax.rsqrt(total / (HEADS * HD) + NORM_EPS)
+            squared = sum(parts[group, at, :, here] for group in range(peers.count))
+            scale = lax.rsqrt(squared / (HEADS * HD) + NORM_EPS)
             scale = jnp.broadcast_to(scale[0:1, :], (HD, HD)).T
             cosine, sine = trig[0, here, :], trig[1, here, :]
             for head in range(heads_here):
@@ -589,7 +676,7 @@
     def multiply_value(at):
         head = head_of(at)
         with mark("v_arrived"):
-            value(at).arrived(2, 3, 4, 7, 8)
+            value(at).arrived_all()
 
         @pl.loop(0, 2)
         @jax.named_scope("v_multiply")
@@ -657,6 +744,8 @@
     with mark("v_near1"):
         value(1).near()
     value(2).begin()
+    with mark("k_forward"):
+        key_halo.forward()
     with mark("q_peers"):
         peers.finish(QUERY)
     with mark("q_rotate"):
@@ -700,8 +789,10 @@
     def relays(at):
         for far in range(line.count - 1):
             from_head = at - 2 - far
-
-            @pl.when((from_head >= 1) & (from_head < heads_here))
+            if isinstance(from_head, int) and from_head >= heads_here:
+                continue
+
+            @pl.when((from_head >= 2) & (from_head < heads_here))
             def _():
                 line.relay(far, from_head)
 
@@ -722,11 +813,21 @@
         for at in range(2):
             peers.sent(at)
         key_halo.sent()
+    with mark("v_far"):
+        value(1).far()
+    multiply_value(1)
+    with mark("v_near"):
+        value(2).near()
     value(3).begin()
+    value(4).begin()
+    make_weights(1)
     with mark("line0"):
         line.relay(0, 0)
-
-    @pl.loop(1, heads_here + 1)
+    with mark("v_halo_relay"):
+        value_halo(1).relay()
+    share(1)
+
+    @pl.loop(2, heads_here + 1)
     def _(at):
         @pl.when(at < heads_here - 1)
         @jax.named_scope("v_near")
@@ -748,7 +849,7 @@
         def _():
             output(0).far()
 
-        @pl.when(at > 1)
+        @pl.when(at > 2)
         def _():
             make_weights(at - 1)
             with mark("v_halo_relay"):
@@ -762,25 +863,21 @@
         def _():
             value(at + DEPTH).begin()
 
-        @pl.when((at >= heads_here - DEPTH) & (at < heads_here - 1))
+        @pl.when(at >= heads_here - DEPTH)
         def _():
             output(at + DEPTH - heads_here).begin()
 
-        @pl.when(at == heads_here - 1)
-        def _():
-            @pl.loop(DEPTH - 1, heads_here)
-            def _(one):
-                output(one).begin()
-
-        @pl.when(at > 1)
+        @pl.when(at > 2)
         def _():
             share(at - 1)
 
-        for far in range(1, line.count - 1):
-            @pl.when(at == far)
-            @jax.named_scope("line0")
-            def _():
-                line.relay(far, 0)
+        for far in range(line.count - 1):
+            for first in range(2):
+                if first + far > 0:
+                    @pl.when(at == far + first + 1)
+                    @jax.named_scope("line0")
+                    def _():
+                        line.relay(far, first)
 
         with mark("v_line_relays"):
             relays(at)
@@ -791,64 +888,87 @@
             result_ref.at[:, slab_of(at)], result_hbm.at[:, slab_of(at)], store.at[at]
         )
 
-    def project(at):
+    def project(at, low, high):
+        some = slice(low * HD, high * HD)
+
         @pl.loop(0, 2)
         @jax.named_scope("project")
         def _(step):
-            total = sum(
+            sum_here = sum(
                 jnp.dot(
-                    mixed[group, pl.ds(step * half_frames, half_frames)].reshape(block, group_width),
-                    held_output[group, :, slab_of(at)],
+                    mixed[group, pl.ds(step * half_frames, half_frames), :, some].reshape(
+                        block, (high - low) * HD
+                    ),
+                    held_output[group, some, slab_of(at)],
                     preferred_element_type=jnp.float32,
                 )
                 for group in range(line.count)
             )
             here = pl.ds(pl.multiple_of(step * block, block), block)
-            result_ref[here, slab_of(at)] = total.astype(result_ref.dtype)
-
-        stored(at).start()
-
-    whole_at = 2
-
-    @pl.loop(0, heads_here)
-    def _(at):
-        @pl.when(at < heads_here - 2)
-        @jax.named_scope("o_near")
-        def _():
-            output(at + 2).near()
-
-        @pl.when(at < heads_here - 1)
-        @jax.named_scope("o_far")
-        def _():
-            output(at + 1).far()
-
-        @pl.when(at <= whole_at)
-        @jax.named_scope("o_line_relays")
-        def _():
-            relays(heads_here + 1 + at)
-
-        with mark("v_sent"):
+            if low > 0:
+                sum_here += total[here, slab_of(at)]
+            if high < heads_here:
+                total[here, slab_of(at)] = sum_here
+            else:
+                result_ref[here, slab_of(at)] = sum_here.astype(result_ref.dtype)
+
+        if high == heads_here:
+            stored(at).start()
+
+    def project_all(first, last, low, high):
+        @pl.loop(first, last)
+        def _(at):
+            project(at, low, high)
+
+    early = 3
+    with mark("o_near"):
+        output(2).near()
+    output(4).begin()
+    with mark("o_line_relays"):
+        relays(heads_here + 1)
+    with mark("o_far"):
+        output(1).far()
+    with mark("o_near"):
+        output(3).near()
+    with mark("o_far"):
+        output(0).arrived_all()
+        output(1).arrived_all()
+    project_all(0, 2, 0, early)
+    with mark("o_line_relays"):
+        relays(heads_here + 2)
+    with mark("o_far"):
+        output(2).far()
+    with mark("o_near"):
+        output(4).near()
+    with mark("o_far"):
+        output(3).far()
+        output(2).arrived_all()
+    project_all(2, 3, 0, early)
+    with mark("v_sent"):
+        @pl.loop(0, heads_here)
+        def _(at):
             value(at).sent()
             value_halo(at).sent()
-        with mark("o_arrived"):
-            output(at).arrived(2, 3, 4, 7, 8)
-
-        @pl.when(at == whole_at)
-        def _():
-            @pl.loop(0, whole_at + 1)
-            def _(one):
-                project(one)
-
-        @pl.when(at > whole_at)
-        def _():
-            project(at)
-
-    with mark("sent"):
-        @pl.loop(0, heads_here)
+
+    with mark("o_line_relays"):
+        relays(heads_here + 3)
+    project_all(0, 3, early, heads_here)
+    with mark("o_far"):
+        output(4).far()
+        output(3).arrived_all()
+    project_all(3, 4, 0, heads_here)
+    with mark("v_sent"):
+        @pl.loop(0, heads_here - 1)
         def _(at):
             output(at).sent()
 
-        line.sent(heads_here)
+    with mark("o_far"):
+        output(4).arrived_all()
+    project_all(4, heads_here, 0, heads_here)
+    output(4).sent()
+
+    with mark("sent"):
+        line.sent()
 
         @pl.loop(0, heads_here)
         def _(at):
@@ -880,6 +1000,7 @@
         out_specs=anywhere,
         scratch_shapes=[
             pltpu.VMEM((count, columns), jnp.bfloat16),
+            pltpu.VMEM((count, columns), jnp.float32),
             pltpu.VMEM(tokens.shape, tokens.dtype),
             pltpu.VMEM((2, CUBE // 2, 2 * rows, width), query_weight.dtype),
             pltpu.VMEM((CUBE // 2, 2 * rows, width), value_weight.dtype),
@@ -894,22 +1015,25 @@
             pltpu.VMEM((frames, area, HD), jnp.bfloat16),
             pltpu.VMEM((groups, frames, area, width), jnp.bfloat16),
             pltpu.VMEM((groups, 2, 8, count), jnp.float32),
+            pltpu.VMEM((frames // 2, WT * side, width), jnp.bfloat16),
             dma((5,)),
             dma((heads_here,)),
+            dma((2, 2)),
             dma((2, 9)),
-            dma((2, 9)),
-            dma((heads_here, 9)),
-            dma((heads_here, 9)),
-            dma((heads_here, 9)),
-            dma((heads_here, 9)),
+            dma((heads_here, 2)),
+            dma((heads_here, 5)),
+            dma((heads_here, 2)),
+            dma((heads_here, 5)),
             dma((2, groups - 1)),
             dma((2, groups - 1)),
-            dma((2, groups - 1, heads_here)),
+            dma((2, groups - 1)),
             dma((2, groups - 1, heads_here)),
             dma((heads_here + 1, 2)),
             dma((heads_here + 1, 2)),
             dma((heads_here + 1, 2, 3)),
             dma((heads_here + 1, 2, 3)),
+            dma((2, 2)),
+            dma((2, 2)),
         ],
         compiler_params=pltpu.CompilerParams(
             collective_id=0, has_side_effects=True, vmem_limit_bytes=60 * 1024 * 1024

time: 156 us -> 151 us (0.968)
  Pallas kernels: 153 us -> 147 us
    pallas_call x1, Pallas kernels: 153 us -> 147 us  [attention_block(): pl.pallas_call(functools.partial(block_kernel, stride, grid_columns, fram...]
where the time goes in v3:
time: 151 us; the launch traced here: 149 us
  Pallas kernels  147 us (97%)
  local copies, waits for them, and re-layouts  2.47 us (2%)
    pallas_call x1, Pallas kernels, attention_block(): pl.pallas_call(functools.partial(block_kernel, stride, grid_columns, fram...  147 us

profile of v3, /device:TPU:4, one launch (start us, length us, event | category | flops | bytes accessed | tf_op | source)
XLA Modules:
  0.0 149.3 jit_solution(12139529476578606952)
XLA Ops:
  0.0 146.8 %attention_block.1 = bf16[512,1280]{1,0:T(8,128)(2,1)} custom-call(bf16[512,5120]{1,0:T(8,128)(2,1)} %bitcast.2, bf16[640,640]{1,0:T(8,128)(2,1)} %query_hbm.1, bf16[640,640]{1,0:T(8,128)(2,1)} %key_hbm.1, bf16[640,640]{1,0:T(8,128)(2,1)} %value_hbm.1, bf16[320,1280]{1,0:T(8,128)(2,1)} %output_hbm.1, f32[640]{0:T(1024)} %query_gain.1, f32[640]{0:T(1024)} %key_gain.1, ...), custom_call_target="tpu_custom_call" | custom-call | tf_op jit(solution)/shard_map/attention_block/pallas_call | solution.py:996
  146.8 2.5 %copy.13 = bf16[1,8,8,8,1280]{4,3,2,1,0:T(8,128)(2,1)} copy(bf16[1,8,8,8,1280]{4,3,2,1,0:T(8,128)(2,1)} %bitcast.3) | data formatting | bytes 2621440
